TPU v7x, 16 devices: a whole 2x2x2 slice. The times are simulated.
16 devices in a mesh: dp: 4 (over z, y), tp: 4 (over x, core).
Axes of the slice: x: 2, y: 2, z: 2, core: 2. Of those that a mesh axis runs over, the one named last changes fastest.
Arguments:
- x: bfloat16 [8, 192, 2560], P('dp', 'tp'), parts along dimension 0
- start: int32 [8], P('dp'), parts along dimension 0
- k_local: bfloat16 [8, 1024, 4, 256], P('dp', None, 'tp'), parts along dimension 0
- v_local: bfloat16 [8, 1024, 4, 256], P('dp', None, 'tp'), parts along dimension 0
- k_global: bfloat16 [8, 12480, 4, 256], P('dp', None, 'tp'), parts along dimension 0
- v_global: bfloat16 [8, 12480, 4, 256], P('dp', None, 'tp'), parts along dimension 0
- norms: float32 [2, 4, 2560], replicated
- w_q: bfloat16 [2, 2560, 2048], P(None, None, 'tp')
- w_k: bfloat16 [2, 2560, 1024], P(None, None, 'tp')
- w_v: bfloat16 [2, 2560, 1024], P(None, None, 'tp')
- w_o: bfloat16 [2, 2048, 2560], P(None, 'tp')
- w_gate: bfloat16 [2, 2560, 10240], P(None, None, 'tp')
- w_up: bfloat16 [2, 2560, 10240], P(None, None, 'tp')
- w_down: bfloat16 [2, 10240, 2560], P(None, 'tp')
Outputs:
- output 1: bfloat16 [8, 192, 2560], P('dp', 'tp'), parts along dimension 0
- output 2: bfloat16 [8, 1024, 4, 256], P('dp', None, 'tp'), parts along dimension 0
- output 3: bfloat16 [8, 1024, 4, 256], P('dp', None, 'tp'), parts along dimension 0
- output 4: bfloat16 [8, 12480, 4, 256], P('dp', None, 'tp'), parts along dimension 0
- output 5: bfloat16 [8, 12480, 4, 256], P('dp', None, 'tp'), parts along dimension 0
There are 4 independent parts. A program takes and returns all parts, laid end to end along the dimension named above; an argument that names none is the same for every part.
All inputs are finite; a program needn't handle non-finite values.
Results may differ from a plain program's by a relative error of at most 0.02.
Values are sent between devices in bfloat16 or wider.
A program may use at most 1 GiB of HBM per device.

v0:
```python
import functools

import jax
import jax.numpy as jnp
import numpy as np
from jax import lax
from jax.experimental import pallas as pl
from jax.experimental.pallas import tpu as pltpu
from jax.sharding import PartitionSpec as P

BF = jnp.bfloat16
F32 = jnp.float32
MESH = pl.DeviceIdType.MESH
NORM_EPS = 1e-6
ROPE_BASE = 10000.0
LOG2E = 1.4426950408889634
S_IN = 1.0 / (50.0 * 16.0)
S_OUT = 50.0 * LOG2E
S_OFF = 36.0 * LOG2E

D = 2560
HALF = 1280
TOK = 192
BLK = 48
HD = 256
WIN = 1024
VMEM_LIMIT = 67000000
TWO = 2
PAIR = range(TWO)


def dot(a, b):
    return jnp.dot(a, b, preferred_element_type=F32)


def dot_t(a, b):
    return lax.dot_general(a, b, (((1,), (1,)), ((), ())), preferred_element_type=F32)


def soft_weights(scores):
    return jnp.exp2(jnp.tanh(scores * S_IN) * S_OUT - S_OFF)


def rope_into(proj, cos, sin, q_dst, k_dst):
    for head, (ref, row) in enumerate(((q_dst, 0), (q_dst, TOK), (k_dst, 0))):
        lead = proj[:, head * HD:head * HD + 128]
        tail = proj[:, head * HD + 128:(head + 1) * HD]
        ref[row:row + TOK, :128] = (lead * cos - tail * sin).astype(BF)
        ref[row:row + TOK, 128:] = (tail * cos + lead * sin).astype(BF)


class Peers:
    def __init__(self):
        dp = lax.axis_index("dp")
        tp = lax.axis_index("tp")
        self.x = tp // 2
        self.c = lax.rem(tp, 2)
        self.mate = (dp, tp + 1 - 2 * self.c)
        self.far = (dp, lax.rem(tp + 2, 4))

    def barrier(self):
        sem = pltpu.get_barrier_semaphore()
        for peer in (self.mate, self.far):
            pl.semaphore_signal(sem, inc=1, device_id=peer, device_id_type=MESH)
        pl.semaphore_wait(sem, 2)


def remote(src, dst, send, recv, peer):
    return pltpu.make_async_remote_copy(src_ref=src, dst_ref=dst, send_sem=send, recv_sem=recv, device_id=peer, device_id_type=MESH)


def norm_rows(act, h, w):
    def body(i, _):
        xb, cb, r = i // 6, (i // 3) % 2, pl.multiple_of((i % 3) * 16, 16)
        rows = act[h, xb, cb, pl.ds(r, 16), :].astype(F32)
        inv = lax.rsqrt(jnp.sum(rows * rows, axis=-1, keepdims=True) * (1.0 / D) + NORM_EPS)
        act[h, xb, cb, pl.ds(r, 16), :] = (rows * inv * w).astype(BF)
        return 0
    lax.fori_loop(0, 12, body, 0)


class Exchange:
    def __init__(self, peers, pbuf, ds, dr, es, er, d_sem, e_sem):
        self.p, self.pbuf, self.ds, self.dr, self.es, self.er = peers, pbuf, ds, dr, es, er
        self.d_sem, self.e_sem = d_sem, e_sem

    def d_copy(self, h, n):
        return remote(self.ds.at[h, n], self.dr.at[h, n], self.d_sem.at[0, h, n], self.d_sem.at[1, h, n], self.p.mate)

    def e_copy(self, h, n):
        return remote(self.es.at[h, n], self.er.at[h, n], self.e_sem.at[0, h, n], self.e_sem.at[1, h, n], self.p.far)

    def give(self, h, n, part):
        self.pbuf[n] = part.reshape(2, 2, BLK, HALF)
        self.ds[h, n] = self.pbuf[n, :, 1 - self.p.c].astype(BF)
        self.d_copy(h, n).start()

    def send(self, h, n):
        copy = self.d_copy(h, n)
        copy.wait_recv()
        self.es[h, n] = (self.pbuf[n, :, self.p.c] + self.dr[h, n].astype(F32)).astype(BF)
        self.e_copy(h, n).start()
        copy.wait_send()

    def take(self, h, xres, w_post, act, w_pre):
        for n in PAIR:
            self.e_copy(h, n).wait()
        c = self.p.c

        def body(i, _):
            xb, r = i // 3, pl.ds(pl.multiple_of((i % 3) * 16, 16), 16)
            ys = [(self.es[h, n, xb, r, :].astype(F32) + self.er[h, n, xb, r, :].astype(F32)).astype(BF).astype(F32) for n in PAIR]
            inv = lax.rsqrt(sum(jnp.sum(y * y, axis=-1, keepdims=True) for y in ys) * (1.0 / D) + NORM_EPS)
            news = []
            for n in PAIR:
                cols = slice(n * HALF, (n + 1) * HALF)
                new = (xres[h, xb, r, cols].astype(F32) + ys[n] * inv * w_post[:, cols]).astype(BF)
                xres[h, xb, r, cols] = new
                news.append(new.astype(F32))
            inv = lax.rsqrt(sum(jnp.sum(v * v, axis=-1, keepdims=True) for v in news) * (1.0 / D) + NORM_EPS)
            for n in PAIR:
                cols = slice(n * HALF, (n + 1) * HALF)
                act[h, xb, c, r, cols] = (news[n] * inv * w_pre[:, cols]).astype(BF)
            return 0
        lax.fori_loop(0, 6, body, 0)


class Final:
    def __init__(self, peers, pbuf, ds, dr, es, er, d_sem, e_sem):
        self.p, self.pbuf, self.ds, self.dr, self.es, self.er = peers, pbuf, ds, dr, es, er
        self.d_sem, self.e_sem = d_sem, e_sem

    d_copy = Exchange.d_copy
    give = Exchange.give

    def e_copy(self, h, n):
        return remote(self.es.at[h, n, 1 - self.p.x], self.er.at[h, n], self.e_sem.at[0, h, n], self.e_sem.at[1, h, n], self.p.far)

    send = Exchange.send

    def take(self, h, xres, w_post, out):
        for n in PAIR:
            self.e_copy(h, n).wait()
        x = self.p.x

        def body(i, _):
            r = pl.ds(pl.multiple_of(i * 16, 16), 16)
            ys = [(self.es[h, n, x, r, :].astype(F32) + self.er[h, n, r, :].astype(F32)).astype(BF).astype(F32) for n in PAIR]
            inv = lax.rsqrt(sum(jnp.sum(y * y, axis=-1, keepdims=True) for y in ys) * (1.0 / D) + NORM_EPS)
            for n in PAIR:
                cols = slice(n * HALF, (n + 1) * HALF)
                out[h, r, cols] = (xres[h, x, r, cols].astype(F32) + ys[n] * inv * w_post[:, cols]).astype(BF)
            return 0
        lax.fori_loop(0, 3, body, 0)


class Shared:
    def __init__(self, peers, act, sem):
        self.p, self.act, self.sem = peers, act, sem

    def copy(self, h):
        view = self.act.at[h, :, self.p.c]
        return remote(view, view, self.sem.at[0, h], self.sem.at[1, h], self.p.mate)


def load(src, dst, sem):
    copy = pltpu.make_async_copy(src, dst, sem)
    copy.start()
    return copy


def load_mlp(layer, w, buf, sems):
    return [load(w.at[layer, :, pl.ds(n * HALF, HALF)], buf.at[n], sems.at[n]) for n in PAIR]


def gate_up(act, h, wg, wu, hid):
    def body(n, _):
        g = act[h].reshape(TOK, D)
        gate = dot(g, wg[n])
        up = dot(g, wu[n])
        hid[n] = (jax.nn.gelu(gate, approximate=True) * up).astype(BF)
        return 0
    lax.fori_loop(0, 2, body, 0)


def down(hid, wd, n):
    return dot(hid[0], wd[n, :HALF]) + dot(hid[1], wd[n, HALF:])


def first_kernel(start, invf, norms, x_in, kl, vl, wq, wk, wv, wo, wg, wu, wd,
                 q1_out, k1_out, v1_out, xres_out, k0_out, v0_out,
                 act, xres, kc, vc, qs, ks, vs, obuf, hid, pbuf, ds, dr, es, er, wgb, wub, wdb, cosb, sinb, q1s,
                 ag_sem, d_sem, e_sem, g_sem, w_sem, o_sem):
    p = Peers()
    loads = [load(wq.at[0], wdb.at[0, :, pl.ds(0, 512)], w_sem.at[0]),
             load(wk.at[0], wdb.at[0, :, pl.ds(512, 256)], w_sem.at[1]),
             load(wv.at[0], wdb.at[0, :, pl.ds(768, 256)], w_sem.at[2]),
             load(kl, kc, w_sem.at[3]),
             load(vl, vc, w_sem.at[4])]
    load_o = [load(wo.at[0, :, pl.ds(n * HALF, HALF)], wdb.at[1, pl.ds(n * 512, 512), :], w_sem.at[5 + n]) for n in PAIR]
    own = [load(x_in.at[h], act.at[h, p.x, p.c], w_sem.at[7 + h]) for h in PAIR]
    p.barrier()

    def ag_mate(h):
        return remote(x_in.at[h], act.at[h, p.x, p.c], ag_sem.at[0, 0, h], ag_sem.at[0, 1, h], p.mate)

    def ag_far(h):
        return remote(x_in.at[h], act.at[h, p.x, p.c], ag_sem.at[1, 0, h], ag_sem.at[1, 1, h], p.far)

    def ag_pass(h):
        view = act.at[h, 1 - p.x, p.c]
        return remote(view, view, ag_sem.at[2, 0, h], ag_sem.at[2, 1, h], p.mate)

    for h in PAIR:
        ag_far(h).start()
        ag_mate(h).start()
    for h in PAIR:
        pos = (lax.broadcasted_iota(jnp.int32, (TOK, 128), 0) + start[h]).astype(F32)
        angle = pos * invf[...]
        cosb[h] = jnp.cos(angle)
        sinb[h] = jnp.sin(angle)

    w0 = 1.0 + norms[0]
    w1 = 1.0 + norms[1]

    def ag_arrive(h):
        ag_far(h).wait_recv()
        ag_pass(h).start()

    def ag_finish(h):
        own[h].wait()
        ag_mate(h).wait_recv()
        ag_pass(h).wait()
        ag_mate(h).wait_send()
        ag_far(h).wait_send()
        xres[h] = act[h, :, p.c]
        norm_rows(act, h, w0[0:1])

    def local_attention(h):
        q = qs[...]
        row = lax.broadcasted_iota(jnp.int32, (2 * TOK, 1), 0)
        i = jnp.where(row >= TOK, row - TOK, row)
        least = jnp.maximum(i + 1, WIN - start[h])
        acc = jnp.zeros((2 * TOK, HD), F32)
        total = jnp.zeros((2 * TOK, 1), F32)
        for b in PAIR:
            slot = lax.broadcasted_iota(jnp.int32, (1, 512), 1) + b * 512
            age = jnp.bitwise_and(slot - start[h], WIN - 1)
            wts = jnp.where(age >= least, soft_weights(dot_t(q, kc[h, b * 512:(b + 1) * 512, :])), 0.0)
            total += jnp.sum(wts, axis=-1, keepdims=True)
            acc += dot(wts.astype(BF), vc[h, b * 512:(b + 1) * 512, :])
        key = lax.broadcasted_iota(jnp.int32, (1, TOK), 1)
        wts = jnp.where(key <= i, soft_weights(dot_t(q, ks[h])), 0.0)
        total += jnp.sum(wts, axis=-1, keepdims=True)
        acc += dot(wts.astype(BF), vs[h])
        o = (acc / total).astype(BF)
        obuf[:, :HD] = o[:TOK]
        obuf[:, HD:] = o[TOK:]

    ex = [Exchange(p, pbuf, ds, dr, es, er.at[s], d_sem.at[s], e_sem.at[s]) for s in PAIR]
    sh = [Shared(p, act, g_sem.at[s]) for s in PAIR]

    for h in PAIR:
        if h == 0:
            ag_arrive(0)
        ag_finish(h)
        if h == 0:
            for copy in loads + load_o:
                copy.wait()
            load_g = load_mlp(0, wg, wgb, w_sem.at[pl.ds(9, 2)])
            load_u = load_mlp(0, wu, wub, w_sem.at[pl.ds(11, 2)])
        proj = dot(act[h].reshape(TOK, D), wdb[0, :, :1024])
        rope_into(proj, cosb[h], sinb[h], qs, ks.at[h])
        vs[h] = proj[:, 768:].astype(BF)
        local_attention(h)
        for n in PAIR:
            ex[0].give(h, n, dot(obuf[...], wdb[1, n * 512:(n + 1) * 512, :]))
        if h == 0:
            ag_arrive(1)
        for n in PAIR:
            ex[0].send(h, n)
    load_d = load_mlp(0, wd, wdb, w_sem.at[pl.ds(13, 2)])
    outs = [load(ks, k0_out, o_sem.at[0]), load(vs, v0_out, o_sem.at[1])]

    def mlp(h, _):
        ex[0].take(h, xres, w0[1:2], act, w0[2:3])
        sh[0].copy(h).start()

        @pl.when(h == 1)
        def _():
            ex[1].send(0, 1)

        sh[0].copy(h).wait()

        @pl.when(h == 0)
        def _():
            for copy in load_g + load_u:
                copy.wait()

        gate_up(act, h, wgb, wub, hid)

        @pl.when(h == 0)
        def _():
            for copy in load_d:
                copy.wait()

        for n in PAIR:
            ex[1].give(h, n, down(hid, wdb, n))
        ex[1].send(h, 0)
        return 0

    lax.fori_loop(0, 2, mlp, 0)
    loads = [load(wq.at[1], wgb.at[0, :, pl.ds(0, 512)], w_sem.at[15]),
             load(wk.at[1], wgb.at[0, :, pl.ds(512, 256)], w_sem.at[16]),
             load(wv.at[1], wgb.at[0, :, pl.ds(768, 256)], w_sem.at[17])]
    ex[1].take(0, xres, w0[3:4], act, w1[0:1])
    sh[1].copy(0).start()
    ex[1].send(1, 1)
    for copy in outs:
        copy.wait()
    for h in PAIR:
        if h == 1:
            ex[1].take(1, xres, w0[3:4], act, w1[0:1])
            sh[1].copy(1).start()
            outs = [load(xres, xres_out, o_sem.at[2])]
        sh[1].copy(h).wait()
        if h == 0:
            for copy in loads:
                copy.wait()
        proj = dot(act[h].reshape(TOK, D), wgb[0, :, :1024])
        rope_into(proj, cosb[h], sinb[h], q1s.at[h], ks.at[h])
        vs[h] = proj[:, 768:].astype(BF)
    outs += [load(q1s, q1_out, o_sem.at[3]), load(ks, k1_out, o_sem.at[4]), load(vs, v1_out, o_sem.at[5])]
    for copy in outs:
        copy.wait()


def last_kernel(norms, o_in, x_in, wo, wg, wu, wd, out_ref,
                act, xres, obuf, hid, pbuf, ds, dr, es, er, fr, wob, wgb, wub, wdb,
                d_sem, e_sem, g_sem, w_sem):
    p = Peers()
    load_in = [load(o_in, obuf, w_sem.at[0]), load(x_in, xres, w_sem.at[1])]
    load_o = [load(wo.at[1, :, pl.ds(n * HALF, HALF)], wob.at[n], w_sem.at[2 + n]) for n in PAIR]
    p.barrier()
    w1 = 1.0 + norms[1]
    first = Exchange(p, pbuf, ds, dr, es, er, d_sem.at[0], e_sem.at[0])
    final = Final(p, pbuf, ds, dr, es, fr, d_sem.at[1], e_sem.at[1])
    sh = Shared(p, act, g_sem)
    for copy in load_in + load_o:
        copy.wait()
    load_g = load_mlp(1, wg, wgb, w_sem.at[pl.ds(4, 2)])
    load_u = load_mlp(1, wu, wub, w_sem.at[pl.ds(6, 2)])
    load_d = load_mlp(1, wd, wdb, w_sem.at[pl.ds(8, 2)])
    for h in PAIR:
        for n in PAIR:
            first.give(h, n, dot(obuf[h], wob[n]))
        for n in PAIR:
            first.send(h, n)

    def mlp(h, _):
        first.take(h, xres, w1[1:2], act, w1[2:3])
        sh.copy(h).start()

        @pl.when(h == 1)
        def _():
            final.send(0, 1)

        sh.copy(h).wait()

        @pl.when(h == 0)
        def _():
            for copy in load_g + load_u:
                copy.wait()

        gate_up(act, h, wgb, wub, hid)

        @pl.when(h == 0)
        def _():
            for copy in load_d:
                copy.wait()

        for n in PAIR:
            final.give(h, n, down(hid, wdb, n))
        final.send(h, 0)
        return 0

    lax.fori_loop(0, 2, mlp, 0)
    final.send(1, 1)
    final.take(0, xres, w1[3:4], out_ref)
    final.take(1, xres, w1[3:4], out_ref)


def shifted(ref, off, n):
    base = pl.multiple_of((off // 8) * 8, 8)
    rows = ref[pl.ds(base, n + 8), :]
    return pltpu.roll(rows, lax.rem(n + 8 - (off - base), n + 8), 0)[:n]


TILE = 1024
PAST = 12288
CACHE = PAST + TOK
NT = PAST // TILE
WROWS = TOK + 16
AHEAD = 8
HIDE = 1e6


def global_kernel(start, q_in, k_new, v_new, k0_new, v0_new, kl, vl, kg, vg,
                  o_out, kl_out, vl_out, kg_out, vg_out,
                  kb, vb, kt, vt, kwin, vwin, lbuf, ext, pa, pb, acc, tot, obuf, in_sem, out_sem, t_sem, w_sem, l_sem):
    caches = ((kg, kb, kg_out, kt, kwin, k_new), (vg, vb, vg_out, vt, vwin, v_new))
    steps = TWO * NT

    def rows_of(ref, g):
        return ref.at[g // NT, pl.ds(pl.multiple_of(lax.rem(g, NT) * TILE, TILE), TILE)]

    def tile_in(a, g):
        return pltpu.make_async_copy(rows_of(caches[a][0], g), caches[a][1].at[g], in_sem.at[a, g])

    def tile_out(a, g):
        return pltpu.make_async_copy(caches[a][1].at[g], rows_of(caches[a][2], g), out_sem.at[a, g])

    def tail_in(a, h):
        return pltpu.make_async_copy(caches[a][0].at[h, pl.ds(PAST, TOK)], caches[a][3].at[h], t_sem.at[0, a, h])

    def tail_out(a, h):
        return pltpu.make_async_copy(caches[a][3].at[h], caches[a][2].at[h, pl.ds(PAST, TOK)], t_sem.at[1, a, h])

    def win_at(h):
        s = start[h]
        return pl.multiple_of(jnp.minimum((s // 16) * 16, CACHE - WROWS), 16)

    def win_in(a, h):
        return pltpu.make_async_copy(caches[a][0].at[h, pl.ds(win_at(h), WROWS)], caches[a][4].at[h], w_sem.at[0, a, h])

    def win_out(a, h):
        return pltpu.make_async_copy(caches[a][4].at[h], caches[a][2].at[h, pl.ds(win_at(h), WROWS)], w_sem.at[1, a, h])

    local = ((kl, k0_new, kl_out), (vl, v0_new, vl_out))
    for a in PAIR:
        pltpu.make_async_copy(local[a][0], lbuf.at[a], l_sem.at[a]).start()
    for g in range(AHEAD):
        for a in PAIR:
            tile_in(a, g).start()
    for h in PAIR:
        for a in PAIR:
            win_in(a, h).start()
            tail_in(a, h).start()

    for a in PAIR:
        pltpu.make_async_copy(local[a][0], lbuf.at[a], l_sem.at[a]).wait()
        for h in PAIR:
            fresh = local[a][1][h].astype(F32)
            ext[0:TOK] = fresh
            ext[WIN:WIN + TOK] = fresh
            off = jnp.bitwise_and(-start[h], WIN - 1)

            def slots(b, _):
                rows = shifted(ext, off + b * 128, 128)
                age = jnp.bitwise_and(lax.broadcasted_iota(jnp.int32, (128, 1), 0) + (b * 128 + off), WIN - 1)
                at = pl.ds(pl.multiple_of(b * 128, 128), 128)
                lbuf[a, h, at, :] = jnp.where(age < TOK, rows, lbuf[a, h, at, :].astype(F32)).astype(BF)
                return 0

            lax.fori_loop(0, 8, slots, 0)
        pltpu.make_async_copy(lbuf.at[a], local[a][2], l_sem.at[a]).start()

    row = lax.broadcasted_iota(jnp.int32, (2 * TOK, 1), 0)
    qi = jnp.where(row >= TOK, row - TOK, row)

    def fetch(g):
        for a in PAIR:
            tile_in(a, g).wait()
            tile_out(a, g).start()

        @pl.when(g + AHEAD < steps)
        def _():
            for a in PAIR:
                tile_in(a, g + AHEAD).start()

    for h in PAIR:
        acc[...] = jnp.zeros_like(acc)
        tot[...] = jnp.zeros_like(tot)
        pb[...] = jnp.zeros_like(pb)
        base = h * NT

        def weigh(t, dst):
            for b in range(TILE // 256):
                scores = dot_t(q_in[h], kb[base + t, b * 256:(b + 1) * 256, :])
                slot = lax.broadcasted_iota(jnp.int32, (1, 256), 1) + (t * TILE + b * 256)
                off = jnp.where(slot < start[h], S_OFF, HIDE)
                wts = jnp.exp2(jnp.tanh(scores * S_IN) * S_OUT - off)
                tot[...] += wts[:, :128] + wts[:, 128:]
                dst[:, b * 256:(b + 1) * 256] = wts.astype(BF)

        def two_tiles(i, _):
            t = 2 * i
            fetch(base + t)
            fetch(base + t + 1)
            before = dot(pb[...], vb[base + jnp.maximum(t - 1, 0)])
            weigh(t, pa)
            now = dot(pa[...], vb[base + t])
            acc[...] += before + now
            weigh(t + 1, pb)
            return 0

        pairs = (start[h] + 2 * TILE - 1) // (2 * TILE)
        lax.fori_loop(0, pairs, two_tiles, 0)
        lax.fori_loop(2 * pairs, NT, lambda t, _: (fetch(base + t), 0)[1], 0)
        before = dot(pb[...], vb[base + 2 * pairs - 1])
        wts = jnp.where(lax.broadcasted_iota(jnp.int32, (1, TOK), 1) <= qi, soft_weights(dot_t(q_in[h], k_new[h])), 0.0)
        total = jnp.sum(tot[...], axis=-1, keepdims=True) + jnp.sum(wts, axis=-1, keepdims=True)
        o = ((acc[...] + before + dot(wts.astype(BF), v_new[h])) / total).astype(BF)
        obuf[h, :, :HD] = o[:TOK]
        obuf[h, :, HD:] = o[TOK:]

        for a in PAIR:
            tail_in(a, h).wait()
            tail_out(a, h).start()
            win_in(a, h).wait()
            ext[16:16 + TOK] = caches[a][5][h].astype(F32)
            shift = win_at(h) - start[h]
            rows = shifted(ext, shift + 16, WROWS)
            idx = lax.broadcasted_iota(jnp.int32, (WROWS, 1), 0) + shift
            win = caches[a][4]
            win[h] = jnp.where((idx >= 0) & (idx < TOK), rows, win[h].astype(F32)).astype(BF)

    done = pltpu.make_async_copy(obuf, o_out, l_sem.at[2])
    done.start()

    def drain(g, _):
        for a in PAIR:
            tile_out(a, g).wait()
        return 0

    lax.fori_loop(0, steps, drain, 0)
    for h in PAIR:
        for a in PAIR:
            tail_out(a, h).wait()
            win_out(a, h).start()
    done.wait()
    for a in PAIR:
        pltpu.make_async_copy(lbuf.at[a], local[a][2], l_sem.at[a]).wait()
        for h in PAIR:
            win_out(a, h).wait()


ANY = pl.BlockSpec(memory_space=pl.ANY)
VM = pl.BlockSpec(memory_space=pltpu.VMEM)
SM = pl.BlockSpec(memory_space=pltpu.SMEM)
DMA = pltpu.SemaphoreType.DMA


def vmem(*shape, dtype=BF):
    return pltpu.VMEM(shape, dtype)


def sds(*shape, dtype=BF):
    return jax.ShapeDtypeStruct(shape, dtype)


def run_first(start, invf, norms, x, kl, vl, *weights):
    return pl.pallas_call(
        first_kernel,
        name="first",
        out_shape=(sds(TWO, TWO * TOK, HD), sds(TWO, TOK, HD), sds(TWO, TOK, HD), sds(TWO, TWO, BLK, D), sds(TWO, TOK, HD), sds(TWO, TOK, HD)),
        in_specs=[SM, VM, VM] + [ANY] * 10,
        out_specs=(ANY,) * 6,
        scratch_shapes=[
            vmem(TWO, TWO, TWO, BLK, D), vmem(TWO, TWO, BLK, D), vmem(TWO, WIN, HD), vmem(TWO, WIN, HD), vmem(TWO * TOK, HD), vmem(TWO, TOK, HD), vmem(TWO, TOK, HD),
            vmem(TOK, 512), vmem(TWO, TOK, HALF), vmem(TWO, TWO, TWO, BLK, HALF, dtype=F32),
            vmem(TWO, TWO, TWO, BLK, HALF), vmem(TWO, TWO, TWO, BLK, HALF), vmem(TWO, TWO, TWO, BLK, HALF), vmem(TWO, TWO, TWO, TWO, BLK, HALF),
            vmem(TWO, D, HALF), vmem(TWO, D, HALF), vmem(TWO, D, HALF),
            vmem(TWO, TOK, 128, dtype=F32), vmem(TWO, TOK, 128, dtype=F32), vmem(TWO, TWO * TOK, HD),
            DMA((3, TWO, TWO)), DMA((TWO, TWO, TWO, TWO)), DMA((TWO, TWO, TWO, TWO)), DMA((TWO, TWO, TWO)), DMA((18,)), DMA((6,)),
        ],
        compiler_params=pltpu.CompilerParams(collective_id=0, has_side_effects=True, vmem_limit_bytes=VMEM_LIMIT),
    )(start, invf, norms, x, kl, vl, *weights)


def run_global(start, q, k_new, v_new, k0_new, v0_new, kl, vl, kg, vg):
    return pl.pallas_call(
        global_kernel,
        name="attend",
        out_shape=(sds(TWO, TOK, 512), sds(TWO, WIN, HD), sds(TWO, WIN, HD), sds(TWO, CACHE, HD), sds(TWO, CACHE, HD)),
        in_specs=[SM] + [VM] * 5 + [ANY] * 4,
        out_specs=(ANY,) * 5,
        scratch_shapes=[
            vmem(TWO * NT, TILE, HD), vmem(TWO * NT, TILE, HD), vmem(TWO, TOK, HD), vmem(TWO, TOK, HD), vmem(TWO, WROWS, HD), vmem(TWO, WROWS, HD),
            vmem(TWO, TWO, WIN, HD), vmem(TWO * WIN + 8, HD, dtype=F32), vmem(TWO * TOK, TILE), vmem(TWO * TOK, TILE), vmem(TWO * TOK, HD, dtype=F32),
            vmem(TWO * TOK, 128, dtype=F32), vmem(TWO, TOK, 512),
            DMA((TWO, TWO * NT)), DMA((TWO, TWO * NT)), DMA((TWO, TWO, TWO)), DMA((TWO, TWO, TWO)), DMA((3,)),
        ],
        compiler_params=pltpu.CompilerParams(has_side_effects=True, vmem_limit_bytes=VMEM_LIMIT),
    )(start, q, k_new, v_new, k0_new, v0_new, kl, vl, kg, vg)


def run_last(norms, o, x, wo, wg, wu, wd):
    return pl.pallas_call(
        last_kernel,
        name="last",
        out_shape=sds(TWO, BLK, D),
        in_specs=[VM] + [ANY] * 6,
        out_specs=VM,
        scratch_shapes=[
            vmem(TWO, TWO, TWO, BLK, D), vmem(TWO, TWO, BLK, D), vmem(TWO, TOK, 512), vmem(TWO, TOK, HALF), vmem(TWO, TWO, TWO, BLK, HALF, dtype=F32),
            vmem(TWO, TWO, TWO, BLK, HALF), vmem(TWO, TWO, TWO, BLK, HALF), vmem(TWO, TWO, TWO, BLK, HALF), vmem(TWO, TWO, TWO, BLK, HALF), vmem(TWO, TWO, BLK, HALF),
            vmem(TWO, 512, HALF), vmem(TWO, D, HALF), vmem(TWO, D, HALF), vmem(TWO, D, HALF),
            DMA((TWO, TWO, TWO, TWO)), DMA((TWO, TWO, TWO, TWO)), DMA((TWO, TWO)), DMA((10,)),
        ],
        compiler_params=pltpu.CompilerParams(collective_id=1, has_side_effects=True, vmem_limit_bytes=VMEM_LIMIT),
    )(norms, o, x, wo, wg, wu, wd)


def solution(mesh):
    act_spec = P('dp', 'tp', None)
    cache_spec = P('dp', None, 'tp', None)
    col_spec = P(None, None, 'tp')
    row_spec = P(None, 'tp', None)
    arg_specs = (act_spec, P('dp'), cache_spec, cache_spec, cache_spec, cache_spec, P(), col_spec, col_spec, col_spec, row_spec, col_spec, col_spec, row_spec)
    result_specs = (act_spec, cache_spec, cache_spec, cache_spec, cache_spec)
    inv_freq = np.power(np.float64(ROPE_BASE), np.arange(HD // 2) * (-2.0 / HD)).astype(np.float32)[None, :]

    def device_step(x, start, k_local, v_local, k_global, v_global, norms, w_q, w_k, w_v, w_o, w_gate, w_up, w_down):
        def flat(cache):
            return cache.reshape(cache.shape[0], cache.shape[1], cache.shape[3])

        kl, vl, kg, vg = flat(k_local), flat(v_local), flat(k_global), flat(v_global)
        q1, k1, v1, xres, k0, v0 = run_first(start, jnp.asarray(inv_freq), norms, x, kl, vl, w_q, w_k, w_v, w_o, w_gate, w_up, w_down)
        o1, kl_new, vl_new, kg_new, vg_new = run_global(start, q1, k1, v1, k0, v0, kl, vl, kg, vg)
        out = run_last(norms, o1, xres, w_o, w_gate, w_up, w_down)
        return (out, kl_new.reshape(k_local.shape), vl_new.reshape(v_local.shape), kg_new.reshape(k_global.shape), vg_new.reshape(v_global.shape))

    return jax.shard_map(device_step, mesh=mesh, in_specs=arg_specs, out_specs=result_specs, check_vma=False)
```

profile of v0, /device:TPU:0, one launch (start us, length us, event | category | flops | bytes accessed | tf_op | source)
XLA Modules:
  0.0 153.9 jit_solution(13180996379050430711)
XLA Ops:
  0.6 74.0 %first.1 = (bf16[2,384,256]{2,1,0:T(8,128)(2,1)}, bf16[2,192,256]{2,1,0:T(8,128)(2,1)}, bf16[2,192,256]{2,1,0:T(8,128)(2,1)}, bf16[2,2,48,2560]{3,2,1,0:T(8,128)...) custom-call(s32[2]{0:T(128)} %start.3, f32[1,128]{1,0:T(1,128)} %constant.2.clone.invf, ...), custom_call_target="tpu_custom_call" | custom-call | tf_op jit(solution)/shard_map/first/pallas_call | solution.py:563
  74.6 26.0 %attend.1 = (bf16[2,192,512]{2,1,0:T(8,128)(2,1)}, bf16[2,1024,256]{2,1,0:T(8,128)(2,1)}, bf16[2,1024,256]{2,1,0:T(8,128)(2,1)}, bf16[2,12480,256]{2,1,0:T(8,128)(2,1)}, bf16[2,12480,256]{2,1,0:T(8,128)(2,1)}) custom-call(s32[2]{0:T(128)} %start.3, bf16[2,384,256]{2,1,0:T(8,128)(2,1)} %get-tuple-element.16.q_in, ...), custom_call_target="tpu_custom_call" | custom-call | tf_op jit(solution)/shard_map/attend/pallas_call | solution.py:582
  100.6 51.4 %last.1 = bf16[2,48,2560]{2,1,0:T(8,128)(2,1)} custom-call(f32[2,4,2560]{2,1,0:T(4,128)} %norms.3, bf16[2,192,512]{2,1,0:T(8,128)(2,1)} %get-tuple-element.21.o_in, bf16[2,2,48,2560]{3,2,1,0:T(8,128)(2,1)} %get-tuple-element.22.x_in, bf16[2,512,2560]{2,1,0:T(8,128)(2,1)} %wo.3, bf16[2,2560,2560]{2,1,0:T(8,128)(2,1)} %wg.3, bf16[2,2560,2560]{2,1,0:T(8,128)(2,1)} %wu.3, ...), custom_call_target="tpu_custom_call" | custom-call | tf_op jit(solution)/shard_map/last/pallas_call | solution.py:599
  152.0 1.8 %copy.25 = bf16[2,48,2560]{2,1,0:T(8,128)(2,1)} copy(bf16[2,48,2560]{2,1,0:T(8,128)(2,1)} %last.1) | data formatting | bytes 983040
where the time goes:
time: 154 us
  Pallas kernels  151 us (98%)
  local copies, waits for them, and re-layouts  1.84 us (1%)
    pallas_call x1, Pallas kernels, run_first(): pl.pallas_call(first_kernel, name='first', out_shape=(sds(TWO, TWO * TOK,...  74 us
    pallas_call x1, Pallas kernels, run_last(): pl.pallas_call(last_kernel, name='last', out_shape=sds(TWO, BLK, D), in_s...  51.4 us
    pallas_call x1, Pallas kernels, run_global(): pl.pallas_call(global_kernel, name='attend', out_shape=(sds(TWO, TOK, 512...  26 us

commit v1 on v0

v1 whole, which is shorter than its diff:
```python
import functools

import jax
import jax.numpy as jnp
import numpy as np
from jax import lax
from jax.experimental import pallas as pl
from jax.experimental.pallas import tpu as pltpu
from jax.sharding import PartitionSpec as P

BF = jnp.bfloat16
F32 = jnp.float32
MESH = pl.DeviceIdType.MESH
NORM_EPS = 1e-6
ROPE_BASE = 10000.0
LOG2E = 1.4426950408889634
S_IN = 1.0 / (50.0 * 16.0)
S_OUT = 50.0 * LOG2E
S_OFF = 36.0 * LOG2E

D = 2560
HALF = 1280
TOK = 192
BLK = 48
HD = 256
WIN = 1024
VMEM_LIMIT = 67000000
TWO = 2
PAIR = range(TWO)
GROUPS = tuple(slice(i, i + 16) for i in range(0, BLK, 16))


TILE = 1024
PAST = 12288
CACHE = PAST + TOK
NT = PAST // TILE
WROWS = TOK + 16
AHEAD = 5
HIDE = 1e6


def dot(a, b):
    return jnp.dot(a, b, preferred_element_type=F32)


def dot_t(a, b):
    return lax.dot_general(a, b, (((1,), (1,)), ((), ())), preferred_element_type=F32)


def soft_weights(scores):
    return jnp.exp2(jnp.tanh(scores * S_IN) * S_OUT - S_OFF)


def rope_into(proj, cos, sin, q_dst, k_dst):
    for head, (ref, row) in enumerate(((q_dst, 0), (q_dst, TOK), (k_dst, 0))):
        lead = proj[:, head * HD:head * HD + 128]
        tail = proj[:, head * HD + 128:(head + 1) * HD]
        ref[row:row + TOK, :128] = (lead * cos - tail * sin).astype(BF)
        ref[row:row + TOK, 128:] = (tail * cos + lead * sin).astype(BF)


class Peers:
    def __init__(self):
        dp = lax.axis_index("dp")
        tp = lax.axis_index("tp")
        self.x = tp // 2
        self.c = lax.rem(tp, 2)
        self.mate = (dp, tp + 1 - 2 * self.c)
        self.far = (dp, lax.rem(tp + 2, 4))

    def barrier(self):
        sem = pltpu.get_barrier_semaphore()
        for peer in (self.mate, self.far):
            pl.semaphore_signal(sem, inc=1, device_id=peer, device_id_type=MESH)
        pl.semaphore_wait(sem, 2)


def remote(src, dst, send, recv, peer):
    return pltpu.make_async_remote_copy(src_ref=src, dst_ref=dst, send_sem=send, recv_sem=recv, device_id=peer, device_id_type=MESH)


def norm_rows(act, h, w):
    def body(i, _):
        for r in GROUPS:
            rows = act[h, i // 2, i % 2, r, :].astype(F32)
            inv = lax.rsqrt(jnp.sum(rows * rows, axis=-1, keepdims=True) * (1.0 / D) + NORM_EPS)
            act[h, i // 2, i % 2, r, :] = (rows * inv * w).astype(BF)
        return 0
    lax.fori_loop(0, 4, body, 0)


class Exchange:
    def __init__(self, peers, pbuf, ds, dr, es, er, d_sem, e_sem):
        self.p, self.pbuf, self.ds, self.dr, self.es, self.er = peers, pbuf, ds, dr, es, er
        self.d_sem, self.e_sem = d_sem, e_sem

    def d_copy(self, h, n):
        return remote(self.ds.at[h, n], self.dr.at[h, n], self.d_sem.at[0, h, n], self.d_sem.at[1, h, n], self.p.mate)

    def e_copy(self, h, n):
        return remote(self.es.at[h, n], self.er.at[h, n], self.e_sem.at[0, h, n], self.e_sem.at[1, h, n], self.p.far)

    def give(self, h, n, part):
        self.pbuf[n] = part.reshape(2, 2, BLK, HALF)
        self.ds[h, n] = self.pbuf[n, :, 1 - self.p.c].astype(BF)
        self.d_copy(h, n).start()

    def send(self, h, n):
        copy = self.d_copy(h, n)
        copy.wait_recv()
        self.es[h, n] = (self.pbuf[n, :, self.p.c] + self.dr[h, n].astype(F32)).astype(BF)
        self.e_copy(h, n).start()
        copy.wait_send()

    def take(self, h, xres, w_post, act, w_pre):
        for n in PAIR:
            self.e_copy(h, n).wait()
        c = self.p.c

        def body(xb, _):
            for r in GROUPS:
                ys = [(self.es[h, n, xb, r, :].astype(F32) + self.er[h, n, xb, r, :].astype(F32)).astype(BF).astype(F32) for n in PAIR]
                inv = lax.rsqrt(sum(jnp.sum(y * y, axis=-1, keepdims=True) for y in ys) * (1.0 / D) + NORM_EPS)
                news = []
                for n in PAIR:
                    cols = slice(n * HALF, (n + 1) * HALF)
                    new = (xres[h, xb, r, cols].astype(F32) + ys[n] * inv * w_post[:, cols]).astype(BF)
                    xres[h, xb, r, cols] = new
                    news.append(new.astype(F32))
                inv = lax.rsqrt(sum(jnp.sum(v * v, axis=-1, keepdims=True) for v in news) * (1.0 / D) + NORM_EPS)
                for n in PAIR:
                    cols = slice(n * HALF, (n + 1) * HALF)
                    act[h, xb, c, r, cols] = (news[n] * inv * w_pre[:, cols]).astype(BF)
            return 0
        lax.fori_loop(0, 2, body, 0)


class Final:
    def __init__(self, peers, pbuf, ds, dr, es, er, d_sem, e_sem):
        self.p, self.pbuf, self.ds, self.dr, self.es, self.er = peers, pbuf, ds, dr, es, er
        self.d_sem, self.e_sem = d_sem, e_sem

    d_copy = Exchange.d_copy
    give = Exchange.give

    def e_copy(self, h, n):
        return remote(self.es.at[h, n, 1 - self.p.x], self.er.at[h, n, 0], self.e_sem.at[0, h, n], self.e_sem.at[1, h, n], self.p.far)

    send = Exchange.send

    def take(self, h, xres, w_post, out):
        for n in PAIR:
            self.e_copy(h, n).wait()
        x = self.p.x

        for r in GROUPS:
            ys = [(self.es[h, n, x, r, :].astype(F32) + self.er[h, n, 0, r, :].astype(F32)).astype(BF).astype(F32) for n in PAIR]
            inv = lax.rsqrt(sum(jnp.sum(y * y, axis=-1, keepdims=True) for y in ys) * (1.0 / D) + NORM_EPS)
            for n in PAIR:
                cols = slice(n * HALF, (n + 1) * HALF)
                out[h, r, cols] = (xres[h, x, r, cols].astype(F32) + ys[n] * inv * w_post[:, cols]).astype(BF)


class Shared:
    def __init__(self, peers, act, sem):
        self.p, self.act, self.sem = peers, act, sem

    def copy(self, h):
        view = self.act.at[h, :, self.p.c]
        return remote(view, view, self.sem.at[0, h], self.sem.at[1, h], self.p.mate)


def load(src, dst, sem):
    copy = pltpu.make_async_copy(src, dst, sem)
    copy.start()
    return copy


def load_mlp(layer, w, buf, sems):
    return [load(w.at[layer, :, pl.ds(n * HALF, HALF)], buf.at[n], sems.at[n]) for n in PAIR]


def gate_up(act, h, wg, wu, hid):
    def body(n, _):
        g = act[h].reshape(TOK, D)
        gate = dot(g, wg[n])
        up = dot(g, wu[n])
        hid[n] = (jax.nn.gelu(gate, approximate=True) * up).astype(BF)
        return 0
    lax.fori_loop(0, 2, body, 0)


def down(hid, wd, n):
    return dot(hid[0], wd[n, :HALF]) + dot(hid[1], wd[n, HALF:])


def layers_kernel(start, invf, norms, x_in, kl, vl, kg, vg, wq, wk, wv, wo, wg, wu, wd,
                  out_ref, k0_out, v0_out, k1_out, v1_out,
                  act, xres, kc, vc, qs, ks, vs, obuf, hid, pbuf, ds, dr, es, er, wgb, wub, wdb, wob, cosb, sinb, pa, pb, acc, tot,
                  ag_sem, d_sem, e_sem, g_sem, w_sem, o_sem, t_sem):
    p = Peers()
    loads = [load(wq.at[0], wdb.at[0, :, pl.ds(0, 512)], w_sem.at[0]),
             load(wk.at[0], wdb.at[0, :, pl.ds(512, 256)], w_sem.at[1]),
             load(wv.at[0], wdb.at[0, :, pl.ds(768, 256)], w_sem.at[2]),
             load(kl, kc, w_sem.at[3]),
             load(vl, vc, w_sem.at[4])]
    load_o = [load(wo.at[0, :, pl.ds(n * HALF, HALF)], wdb.at[1, pl.ds(n * 512, 512), :], w_sem.at[5 + n]) for n in PAIR]
    own = [load(x_in.at[h], act.at[h, p.x, p.c], w_sem.at[7 + h]) for h in PAIR]
    p.barrier()

    def ag_mate(h):
        return remote(x_in.at[h], act.at[h, p.x, p.c], ag_sem.at[0, 0, h], ag_sem.at[0, 1, h], p.mate)

    def ag_far(h):
        return remote(x_in.at[h], act.at[h, p.x, p.c], ag_sem.at[1, 0, h], ag_sem.at[1, 1, h], p.far)

    def ag_pass(h):
        view = act.at[h, 1 - p.x, p.c]
        return remote(view, view, ag_sem.at[2, 0, h], ag_sem.at[2, 1, h], p.mate)

    for h in PAIR:
        ag_far(h).start()
        ag_mate(h).start()
    for h in PAIR:
        pos = (lax.broadcasted_iota(jnp.int32, (TOK, 128), 0) + start[h]).astype(F32)
        angle = pos * invf[...]
        cosb[h] = jnp.cos(angle)
        sinb[h] = jnp.sin(angle)

    w0 = 1.0 + norms[0]
    w1 = 1.0 + norms[1]

    def ag_arrive(h):
        ag_far(h).wait_recv()
        ag_pass(h).start()

    def ag_finish(h):
        own[h].wait()
        ag_mate(h).wait_recv()
        ag_pass(h).wait()
        ag_mate(h).wait_send()
        ag_far(h).wait_send()
        xres[h] = act[h, :, p.c]
        norm_rows(act, h, w0[0:1])

    def local_attention(h):
        q = qs[...]
        row = lax.broadcasted_iota(jnp.int32, (2 * TOK, 1), 0)
        i = jnp.where(row >= TOK, row - TOK, row)
        least = jnp.maximum(i + 1, WIN - start[h])
        acc = jnp.zeros((2 * TOK, HD), F32)
        total = jnp.zeros((2 * TOK, 1), F32)
        for b in PAIR:
            slot = lax.broadcasted_iota(jnp.int32, (1, 512), 1) + b * 512
            age = jnp.bitwise_and(slot - start[h], WIN - 1)
            wts = jnp.where(age >= least, soft_weights(dot_t(q, kc[h, b * 512:(b + 1) * 512, :])), 0.0)
            total += jnp.sum(wts, axis=-1, keepdims=True)
            acc += dot(wts.astype(BF), vc[h, b * 512:(b + 1) * 512, :])
        key = lax.broadcasted_iota(jnp.int32, (1, TOK), 1)
        wts = jnp.where(key <= i, soft_weights(dot_t(q, ks[h])), 0.0)
        total += jnp.sum(wts, axis=-1, keepdims=True)
        acc += dot(wts.astype(BF), vs[h])
        o = (acc / total).astype(BF)
        obuf[:, :HD] = o[:TOK]
        obuf[:, HD:] = o[TOK:]

    ex = [Exchange(p, pbuf, ds, dr, es, er.at[s % 2], d_sem.at[s], e_sem.at[s]) for s in range(3)]
    ex.append(Final(p, pbuf, ds, dr, es, er.at[1], d_sem.at[3], e_sem.at[3]))
    sh = [Shared(p, act, g_sem.at[s]) for s in range(3)]

    for h in PAIR:
        if h == 0:
            ag_arrive(0)
        ag_finish(h)
        if h == 0:
            for copy in loads + load_o:
                copy.wait()
            load_g = load_mlp(0, wg, wgb, w_sem.at[pl.ds(9, 2)])
            load_u = load_mlp(0, wu, wub, w_sem.at[pl.ds(11, 2)])
        proj = dot(act[h].reshape(TOK, D), wdb[0, :, :1024])
        rope_into(proj, cosb[h], sinb[h], qs, ks.at[h])
        vs[h] = proj[:, 768:].astype(BF)
        local_attention(h)
        for n in PAIR:
            ex[0].give(h, n, dot(obuf[...], wdb[1, n * 512:(n + 1) * 512, :]))
        if h == 0:
            ag_arrive(1)
        for n in PAIR:
            ex[0].send(h, n)
    load_d = load_mlp(0, wd, wdb, w_sem.at[pl.ds(13, 2)])
    outs = [load(ks, k0_out, o_sem.at[0]), load(vs, v0_out, o_sem.at[1])]

    def mlp(before, after, share, w_post, w_pre, first_loads, last_loads):
        def body(h, _):
            before.take(h, xres, w_post, act, w_pre)
            share.copy(h).start()

            @pl.when(h == 1)
            def _():
                after.send(0, 1)

            share.copy(h).wait()

            @pl.when(h == 0)
            def _():
                for copy in first_loads:
                    copy.wait()

            gate_up(act, h, wgb, wub, hid)

            @pl.when(h == 0)
            def _():
                for copy in last_loads:
                    copy.wait()

            for n in PAIR:
                after.give(h, n, down(hid, wdb, n))
            after.send(h, 0)
            return 0

        lax.fori_loop(0, 2, body, 0)

    mlp(ex[0], ex[1], sh[0], w0[1:2], w0[2:3], load_g + load_u, load_d)

    loads = [load(wq.at[1], wgb.at[0, :, pl.ds(0, 512)], w_sem.at[15]),
             load(wk.at[1], wgb.at[0, :, pl.ds(512, 256)], w_sem.at[16]),
             load(wv.at[1], wgb.at[0, :, pl.ds(768, 256)], w_sem.at[17])]

    def ring(a, g):
        s = lax.rem(g, 8)
        return wdb.at[s // 4, pl.ds(a * TILE, TILE), pl.ds(pl.multiple_of(lax.rem(s, 4) * HD, HD), HD)]

    def tile_in(a, g):
        src = (kg, vg)[a].at[g // NT, pl.ds(pl.multiple_of(lax.rem(g, NT) * TILE, TILE), TILE)]
        return pltpu.make_async_copy(src, ring(a, g), t_sem.at[a, g])

    for g in range(AHEAD):
        for a in PAIR:
            tile_in(a, g).start()
    load_o1 = [load(wo.at[1, :, pl.ds(n * HALF, HALF)], wob.at[n], w_sem.at[18 + n]) for n in PAIR]
    load_u1 = load_mlp(1, wu, wub, w_sem.at[pl.ds(11, 2)])
    load_g1 = [pltpu.make_async_copy(wg.at[1, :, pl.ds(n * HALF, HALF)], wgb.at[n], w_sem.at[9 + n]) for n in PAIR]

    def fetch(g):
        for a in PAIR:
            tile_in(a, g).wait()

        @pl.when(g + AHEAD < TWO * NT)
        def _():
            for a in PAIR:
                tile_in(a, g + AHEAD).start()

    row = lax.broadcasted_iota(jnp.int32, (2 * TOK, 1), 0)
    qi = jnp.where(row >= TOK, row - TOK, row)

    def global_attention(h):
        acc[...] = jnp.zeros_like(acc)
        tot[...] = jnp.zeros_like(tot)
        pb[...] = jnp.zeros_like(pb)
        base = h * NT

        def weigh(t, dst):
            keys = ring(0, base + t)
            for b in range(TILE // 256):
                scores = dot_t(qs[...], keys[b * 256:(b + 1) * 256, :])
                slot = lax.broadcasted_iota(jnp.int32, (1, 256), 1) + (t * TILE + b * 256)
                off = jnp.where(slot < start[h], S_OFF, HIDE)
                wts = jnp.exp2(jnp.tanh(scores * S_IN) * S_OUT - off)
                tot[...] += wts[:, :128] + wts[:, 128:]
                dst[:, b * 256:(b + 1) * 256] = wts.astype(BF)

        def two_tiles(i, _):
            t = 2 * i
            fetch(base + t)
            fetch(base + t + 1)
            before = dot(pb[...], ring(1, base + jnp.maximum(t - 1, 0))[...])
            weigh(t, pa)
            now = dot(pa[...], ring(1, base + t)[...])
            acc[...] += before + now
            weigh(t + 1, pb)
            return 0

        lax.fori_loop(0, NT // 2, two_tiles, 0)
        before = dot(pb[...], ring(1, base + NT - 1)[...])
        wts = jnp.where(lax.broadcasted_iota(jnp.int32, (1, TOK), 1) <= qi, soft_weights(dot_t(qs[...], ks[h])), 0.0)
        total = jnp.sum(tot[...], axis=-1, keepdims=True) + jnp.sum(wts, axis=-1, keepdims=True)
        o = ((acc[...] + before + dot(wts.astype(BF), vs[h])) / total).astype(BF)
        obuf[:, :HD] = o[:TOK]
        obuf[:, HD:] = o[TOK:]

    def attend(h, _):
        ex[1].take(h, xres, w0[3:4], act, w1[0:1])
        sh[1].copy(h).start()

        @pl.when(h == 0)
        def _():
            ex[1].send(1, 1)
            for copy in outs + loads + load_o1:
                copy.wait()

        sh[1].copy(h).wait()
        proj = dot(act[h].reshape(TOK, D), wgb[0, :, :1024])
        rope_into(proj, cosb[h], sinb[h], qs, ks.at[h])
        vs[h] = proj[:, 768:].astype(BF)

        @pl.when(h == 1)
        def _():
            for copy in load_g1:
                copy.start()

        global_attention(h)
        for n in PAIR:
            ex[2].give(h, n, dot(obuf[...], wob[n]))
        for n in PAIR:
            ex[2].send(h, n)
        return 0

    lax.fori_loop(0, 2, attend, 0)
    outs = [load(ks, k1_out, o_sem.at[2]), load(vs, v1_out, o_sem.at[3])]
    load_d1 = load_mlp(1, wd, wdb, w_sem.at[pl.ds(13, 2)])
    mlp(ex[2], ex[3], sh[2], w1[1:2], w1[2:3], load_u1 + load_g1, load_d1)
    ex[3].send(1, 1)
    for h in PAIR:
        ex[3].take(h, xres, w1[3:4], out_ref)
    for copy in outs:
        copy.wait()


def shifted(ref, off, n):
    base = pl.multiple_of((off // 8) * 8, 8)
    rows = ref[pl.ds(base, n + 8), :]
    return pltpu.roll(rows, lax.rem(n + 8 - (off - base), n + 8), 0)[:n]


def cache_kernel(start, k_new, v_new, k0_new, v0_new, kl, vl, kg, vg,
                 kl_out, vl_out, kg_out, vg_out,
                 kb, vb, kt, vt, kwin, vwin, lbuf, ext, in_sem, out_sem, t_sem, w_sem, l_sem):
    caches = ((kg, kb, kg_out, kt, kwin, k_new), (vg, vb, vg_out, vt, vwin, v_new))
    steps = TWO * NT

    def rows_of(ref, g):
        return ref.at[g // NT, pl.ds(pl.multiple_of(lax.rem(g, NT) * TILE, TILE), TILE)]

    def tile_in(a, g):
        return pltpu.make_async_copy(rows_of(caches[a][0], g), caches[a][1].at[g], in_sem.at[a, g])

    def tile_out(a, g):
        return pltpu.make_async_copy(caches[a][1].at[g], rows_of(caches[a][2], g), out_sem.at[a, g])

    def tail_in(a, h):
        return pltpu.make_async_copy(caches[a][0].at[h, pl.ds(PAST, TOK)], caches[a][3].at[h], t_sem.at[0, a, h])

    def tail_out(a, h):
        return pltpu.make_async_copy(caches[a][3].at[h], caches[a][2].at[h, pl.ds(PAST, TOK)], t_sem.at[1, a, h])

    def win_at(h):
        s = start[h]
        return pl.multiple_of(jnp.minimum((s // 16) * 16, CACHE - WROWS), 16)

    def win_in(a, h):
        return pltpu.make_async_copy(caches[a][0].at[h, pl.ds(win_at(h), WROWS)], caches[a][4].at[h], w_sem.at[0, a, h])

    def win_out(a, h):
        return pltpu.make_async_copy(caches[a][4].at[h], caches[a][2].at[h, pl.ds(win_at(h), WROWS)], w_sem.at[1, a, h])

    local = ((kl, k0_new, kl_out), (vl, v0_new, vl_out))
    for a in PAIR:
        pltpu.make_async_copy(local[a][0], lbuf.at[a], l_sem.at[a]).start()
    for h in PAIR:
        for a in PAIR:
            win_in(a, h).start()
            tail_in(a, h).start()

    def begin(g, _):
        for a in PAIR:
            tile_in(a, g).start()
        return 0

    lax.fori_loop(0, steps, begin, 0)

    def move(g, _):
        for a in PAIR:
            tile_in(a, g).wait()
            tile_out(a, g).start()
        return 0

    def local_rows(a, h):
        fresh = local[a][1][h].astype(F32)
        ext[0:TOK] = fresh
        ext[WIN:WIN + TOK] = fresh
        off = jnp.bitwise_and(-start[h], WIN - 1)

        def slots(b, _):
            lead = jnp.bitwise_and(b * 128 + off, WIN - 1)

            @pl.when((lead < TOK) | (lead > WIN - 128))
            def _():
                rows = shifted(ext, off + b * 128, 128)
                age = jnp.bitwise_and(lax.broadcasted_iota(jnp.int32, (128, 1), 0) + lead, WIN - 1)
                at = pl.ds(pl.multiple_of(b * 128, 128), 128)
                lbuf[a, h, at, :] = jnp.where(age < TOK, rows, lbuf[a, h, at, :].astype(F32)).astype(BF)

            return 0

        lax.fori_loop(0, WIN // 128, slots, 0)

    def global_rows(a, h):
        win_in(a, h).wait()
        ext[16:16 + TOK] = caches[a][5][h].astype(F32)
        shift = win_at(h) - start[h]
        rows = shifted(ext, shift + 16, WROWS)
        idx = lax.broadcasted_iota(jnp.int32, (WROWS, 1), 0) + shift
        win = caches[a][4]
        win[h] = jnp.where((idx >= 0) & (idx < TOK), rows, win[h].astype(F32)).astype(BF)

    for a in PAIR:
        pltpu.make_async_copy(local[a][0], lbuf.at[a], l_sem.at[a]).wait()
        for h in PAIR:
            i = TWO * a + h
            local_rows(a, h)
            lax.fori_loop(i * 3, i * 3 + 3, move, 0)
        pltpu.make_async_copy(lbuf.at[a], local[a][2], l_sem.at[a]).start()
    for a in PAIR:
        for h in PAIR:
            i = TWO * a + h
            tail_in(a, h).wait()
            tail_out(a, h).start()
            global_rows(a, h)
            lax.fori_loop(NT + i * 3, NT + i * 3 + 3, move, 0)

    def drain(g, _):
        for a in PAIR:
            tile_out(a, g).wait()
        return 0

    for h in PAIR:
        lax.fori_loop(h * NT, h * NT + NT, drain, 0)
        for a in PAIR:
            tail_out(a, h).wait()
            win_out(a, h).start()
    for a in PAIR:
        pltpu.make_async_copy(lbuf.at[a], local[a][2], l_sem.at[a]).wait()
        for h in PAIR:
            win_out(a, h).wait()


ANY = pl.BlockSpec(memory_space=pl.ANY)
VM = pl.BlockSpec(memory_space=pltpu.VMEM)
SM = pl.BlockSpec(memory_space=pltpu.SMEM)
DMA = pltpu.SemaphoreType.DMA


def vmem(*shape, dtype=BF):
    return pltpu.VMEM(shape, dtype)


def sds(*shape, dtype=BF):
    return jax.ShapeDtypeStruct(shape, dtype)


def run_layers(start, invf, norms, x, kl, vl, kg, vg, *weights):
    rows = sds(TWO, TOK, HD)
    pieces = vmem(TWO, TWO, TWO, BLK, HALF)
    return pl.pallas_call(
        layers_kernel,
        name="layers",
        out_shape=(sds(TWO, BLK, D), rows, rows, rows, rows),
        in_specs=[SM, VM, VM] + [ANY] * 12,
        out_specs=(VM, ANY, ANY, ANY, ANY),
        scratch_shapes=[
            vmem(TWO, TWO, TWO, BLK, D), vmem(TWO, TWO, BLK, D), vmem(TWO, WIN, HD), vmem(TWO, WIN, HD),
            vmem(TWO * TOK, HD), vmem(TWO, TOK, HD), vmem(TWO, TOK, HD),
            vmem(TOK, 512), vmem(TWO, TOK, HALF), vmem(TWO, TWO, TWO, BLK, HALF, dtype=F32),
            pieces, pieces, pieces, vmem(TWO, TWO, TWO, TWO, BLK, HALF),
            vmem(TWO, D, HALF), vmem(TWO, D, HALF), vmem(TWO, D, HALF), vmem(TWO, 512, HALF),
            vmem(TWO, TOK, 128, dtype=F32), vmem(TWO, TOK, 128, dtype=F32),
            vmem(TWO * TOK, TILE), vmem(TWO * TOK, TILE), vmem(TWO * TOK, HD, dtype=F32), vmem(TWO * TOK, 128, dtype=F32),
            DMA((3, TWO, TWO)), DMA((4, TWO, TWO, TWO)), DMA((4, TWO, TWO, TWO)), DMA((3, TWO, TWO)), DMA((20,)), DMA((4,)),
            DMA((TWO, TWO * NT)),
        ],
        compiler_params=pltpu.CompilerParams(collective_id=0, has_side_effects=True, vmem_limit_bytes=VMEM_LIMIT),
    )(start, invf, norms, x, kl, vl, kg, vg, *weights)


def run_caches(start, k_new, v_new, k0_new, v0_new, kl, vl, kg, vg):
    tiles = vmem(TWO * NT, TILE, HD)
    window = vmem(TWO, WROWS, HD)
    return pl.pallas_call(
        cache_kernel,
        name="caches",
        out_shape=(sds(TWO, WIN, HD), sds(TWO, WIN, HD), sds(TWO, CACHE, HD), sds(TWO, CACHE, HD)),
        in_specs=[SM] + [VM] * 4 + [ANY] * 4,
        out_specs=(ANY,) * 4,
        scratch_shapes=[
            tiles, tiles, vmem(TWO, TOK, HD), vmem(TWO, TOK, HD), window, window,
            vmem(TWO, TWO, WIN, HD), vmem(TWO * WIN + 8, HD, dtype=F32),
            DMA((TWO, TWO * NT)), DMA((TWO, TWO * NT)), DMA((TWO, TWO, TWO)), DMA((TWO, TWO, TWO)), DMA((TWO,)),
        ],
        compiler_params=pltpu.CompilerParams(has_side_effects=True, vmem_limit_bytes=VMEM_LIMIT),
    )(start, k_new, v_new, k0_new, v0_new, kl, vl, kg, vg)


def solution(mesh):
    act_spec = P('dp', 'tp', None)
    cache_spec = P('dp', None, 'tp', None)
    col_spec = P(None, None, 'tp')
    row_spec = P(None, 'tp', None)
    arg_specs = (act_spec, P('dp'), cache_spec, cache_spec, cache_spec, cache_spec, P(), col_spec, col_spec, col_spec, row_spec, col_spec, col_spec, row_spec)
    result_specs = (act_spec, cache_spec, cache_spec, cache_spec, cache_spec)
    inv_freq = np.power(np.float64(ROPE_BASE), np.arange(HD // 2) * (-2.0 / HD)).astype(np.float32)[None, :]

    def device_step(x, start, k_local, v_local, k_global, v_global, norms, w_q, w_k, w_v, w_o, w_gate, w_up, w_down):
        def flat(cache):
            return cache.reshape(cache.shape[0], cache.shape[1], cache.shape[3])

        kl, vl, kg, vg = flat(k_local), flat(v_local), flat(k_global), flat(v_global)
        invf = jnp.asarray(inv_freq)
        out, k0, v0, k1, v1 = run_layers(start, invf, norms, x, kl, vl, kg, vg, w_q, w_k, w_v, w_o, w_gate, w_up, w_down)
        kl_new, vl_new, kg_new, vg_new = run_caches(start, k1, v1, k0, v0, kl, vl, kg, vg)
        return (out, kl_new.reshape(k_local.shape), vl_new.reshape(v_local.shape), kg_new.reshape(k_global.shape), vg_new.reshape(v_global.shape))

    return jax.shard_map(device_step, mesh=mesh, in_specs=arg_specs, out_specs=result_specs, check_vma=False)
```

time: 154 us -> 144 us (0.935)
  Pallas kernels: 151 us -> 141 us
    pallas_call x3 -> x2, Pallas kernels: 151 us -> 141 us  [the longest x1 120 us: run_layers(): pl.pallas_call(layers_kernel, name='layers', out_shape=(sds(TWO, BLK, D),...]
where the time goes in v1:
time: 144 us
  Pallas kernels  141 us (98%)
  local copies, waits for them, and re-layouts  1.84 us (1%)
    pallas_call x1, Pallas kernels, run_layers(): pl.pallas_call(layers_kernel, name='layers', out_shape=(sds(TWO, BLK, D),...  120 us
    pallas_call x1, Pallas kernels, run_caches(): pl.pallas_call(cache_kernel, name='caches', out_shape=(sds(TWO, WIN, HD),...  21.2 us

profile of v1, /device:TPU:0, one launch (start us, length us, event | category | flops | bytes accessed | tf_op | source)
XLA Modules:
  0.0 143.9 jit_solution(13381741342407926574)
XLA Ops:
  0.6 120.2 %layers.1 = (bf16[2,48,2560]{2,1,0:T(8,128)(2,1)}, bf16[2,192,256]{2,1,0:T(8,128)(2,1)}, bf16[2,192,256]{2,1,0:T(8,128)(2,1)}, bf16[2,192,256]{2,1,0:T(8,128)(2,1)}, bf16[2,192,256]{2,1,0:T(8,128)(2,1)}) custom-call(s32[2]{0:T(128)} %start.3, f32[1,128]{1,0:T(1,128)} %constant.2.clone.invf, f32[2,4,2560]{2,1,0:T(4,128)} %norms.1, bf16[2,48,2560]{2,1,0:T(8,128)(2,1)} %x_in.1, ...), custom_call_target="tpu_custom_call" | custom-call | tf_op jit(solution)/shard_map/layers/pallas_call | solution.py:564
  120.8 21.2 %caches.1 = (bf16[2,1024,256]{2,1,0:T(8,128)(2,1)}, bf16[2,1024,256]{2,1,0:T(8,128)(2,1)}, bf16[2,12480,256]{2,1,0:T(8,128)(2,1)}, bf16[2,12480,256]{2,1,0:T(8,128)(2,1)}) custom-call(s32[2]{0:T(128)} %start.3, bf16[2,192,256]{2,1,0:T(8,128)(2,1)} %get-tuple-element.15.k_new, bf16[2,192,256]{2,1,0:T(8,128)(2,1)} %get-tuple-element.16.v_new, ...), custom_call_target="tpu_custom_call" | custom-call | tf_op jit(solution)/shard_map/caches/pallas_call | solution.py:588
  142.0 1.8 %copy.25 = bf16[2,48,2560]{2,1,0:T(8,128)(2,1)} copy(bf16[2,48,2560]{2,1,0:T(8,128)(2,1)} %get-tuple-element.33) | data formatting | bytes 983040

commit v2 on v1

v2 whole, which is shorter than its diff:
```python
import functools

import jax
import jax.numpy as jnp
import numpy as np
from jax import lax
from jax.experimental import pallas as pl
from jax.experimental.pallas import tpu as pltpu
from jax.sharding import PartitionSpec as P

BF = jnp.bfloat16
F32 = jnp.float32
MESH = pl.DeviceIdType.MESH
NORM_EPS = 1e-6
ROPE_BASE = 10000.0
LOG2E = 1.4426950408889634
S_IN = 1.0 / (50.0 * 16.0)
S_OUT = 50.0 * LOG2E
S_OFF = 36.0 * LOG2E

D = 2560
HALF = 1280
TOK = 192
BLK = 48
HD = 256
WIN = 1024
VMEM_LIMIT = 67000000
TWO = 2
PAIR = range(TWO)
GROUPS = tuple(slice(i, i + 16) for i in range(0, BLK, 16))


TILE = 1024
PAST = 12288
CACHE = PAST + TOK
NT = PAST // TILE
WROWS = TOK + 16
AHEAD = 5
HIDE = 1e6


def dot(a, b):
    return jnp.dot(a, b, preferred_element_type=F32)


def dot_t(a, b):
    return lax.dot_general(a, b, (((1,), (1,)), ((), ())), preferred_element_type=F32)


def soft_weights(scores):
    return jnp.exp2(jnp.tanh(scores * S_IN) * S_OUT - S_OFF)


def rope_into(proj, cos, sin, q_dst, k_dst):
    for head, (ref, row) in enumerate(((q_dst, 0), (q_dst, TOK), (k_dst, 0))):
        lead = proj[:, head * HD:head * HD + 128]
        tail = proj[:, head * HD + 128:(head + 1) * HD]
        ref[row:row + TOK, :128] = (lead * cos - tail * sin).astype(BF)
        ref[row:row + TOK, 128:] = (tail * cos + lead * sin).astype(BF)


class Peers:
    def __init__(self):
        dp = lax.axis_index("dp")
        tp = lax.axis_index("tp")
        self.x = tp // 2
        self.c = lax.rem(tp, 2)
        self.mate = (dp, tp + 1 - 2 * self.c)
        self.far = (dp, lax.rem(tp + 2, 4))

    def barrier(self):
        sem = pltpu.get_barrier_semaphore()
        for peer in (self.mate, self.far):
            pl.semaphore_signal(sem, inc=1, device_id=peer, device_id_type=MESH)
        pl.semaphore_wait(sem, 2)


def remote(src, dst, send, recv, peer):
    return pltpu.make_async_remote_copy(src_ref=src, dst_ref=dst, send_sem=send, recv_sem=recv, device_id=peer, device_id_type=MESH)


def norm_rows(act, h, w):
    def body(i, _):
        for r in GROUPS:
            rows = act[h, i // 2, i % 2, r, :].astype(F32)
            inv = lax.rsqrt(jnp.sum(rows * rows, axis=-1, keepdims=True) * (1.0 / D) + NORM_EPS)
            act[h, i // 2, i % 2, r, :] = (rows * inv * w).astype(BF)
        return 0
    lax.fori_loop(0, 4, body, 0)


class Exchange:
    def __init__(self, peers, pbuf, ds, dr, es, er, d_sem, e_sem, final=None):
        self.p, self.pbuf, self.ds, self.dr, self.es, self.er = peers, pbuf, ds, dr, es, er
        self.d_sem, self.e_sem, self.final = d_sem, e_sem, final

    def d_copy(self, h, n):
        return remote(self.ds.at[h, n], self.dr.at[h, n], self.d_sem.at[0, h, n], self.d_sem.at[1, h, n], self.p.mate)

    def e_copy(self, h, n):
        return remote(self.es.at[h, n], self.er.at[h, n], self.e_sem.at[0, h, n], self.e_sem.at[1, h, n], self.p.far)

    def give(self, h, n, part):
        self.pbuf[n] = part.reshape(2, 2, BLK, HALF)
        self.ds[h, n] = self.pbuf[n, :, 1 - self.p.c].astype(BF)
        self.d_copy(h, n).start()

    def send(self, h, n):
        copy = self.d_copy(h, n)
        copy.wait_recv()
        self.es[h, n] = (self.pbuf[n, :, self.p.c] + self.dr[h, n].astype(F32)).astype(BF)
        if self.final is None:
            self.e_copy(h, n).start()
        else:
            pl.when(self.final)(lambda: self.f_copy(h, n).start())
            pl.when(jnp.logical_not(self.final))(lambda: self.e_copy(h, n).start())
        copy.wait_send()

    def f_copy(self, h, n):
        return remote(self.es.at[h, n, 1 - self.p.x], self.er.at[h, n, 0], self.e_sem.at[0, h, n], self.e_sem.at[1, h, n], self.p.far)

    def take(self, h, xres, w_post, act, w_pre):
        for n in PAIR:
            self.e_copy(h, n).wait()
        c = self.p.c

        def body(xb, _):
            for r in GROUPS:
                ys = [(self.es[h, n, xb, r, :].astype(F32) + self.er[h, n, xb, r, :].astype(F32)).astype(BF).astype(F32) for n in PAIR]
                inv = lax.rsqrt(sum(jnp.sum(y * y, axis=-1, keepdims=True) for y in ys) * (1.0 / D) + NORM_EPS)
                news = []
                for n in PAIR:
                    cols = slice(n * HALF, (n + 1) * HALF)
                    new = (xres[h, xb, r, cols].astype(F32) + ys[n] * inv * w_post[:, cols]).astype(BF)
                    xres[h, xb, r, cols] = new
                    news.append(new.astype(F32))
                inv = lax.rsqrt(sum(jnp.sum(v * v, axis=-1, keepdims=True) for v in news) * (1.0 / D) + NORM_EPS)
                for n in PAIR:
                    cols = slice(n * HALF, (n + 1) * HALF)
                    act[h, xb, c, r, cols] = (news[n] * inv * w_pre[:, cols]).astype(BF)
            return 0
        lax.fori_loop(0, 2, body, 0)

    def take_final(self, h, xres, w_post, out):
        for n in PAIR:
            self.f_copy(h, n).wait()
        x = self.p.x

        for r in GROUPS:
            ys = [(self.es[h, n, x, r, :].astype(F32) + self.er[h, n, 0, r, :].astype(F32)).astype(BF).astype(F32) for n in PAIR]
            inv = lax.rsqrt(sum(jnp.sum(y * y, axis=-1, keepdims=True) for y in ys) * (1.0 / D) + NORM_EPS)
            for n in PAIR:
                cols = slice(n * HALF, (n + 1) * HALF)
                out[h, r, cols] = (xres[h, x, r, cols].astype(F32) + ys[n] * inv * w_post[:, cols]).astype(BF)


class Shared:
    def __init__(self, peers, act, sem):
        self.p, self.act, self.sem = peers, act, sem

    def copy(self, h):
        view = self.act.at[h, :, self.p.c]
        return remote(view, view, self.sem.at[0, h], self.sem.at[1, h], self.p.mate)


def load(src, dst, sem):
    copy = pltpu.make_async_copy(src, dst, sem)
    copy.start()
    return copy


def gate_up(act, h, wg, wu, hid, between=None):
    def body(n, _):
        if between is not None:
            pl.when(n == 1)(between)
        g = act[h].reshape(TOK, D)
        gate = dot(g, wg[n])
        up = dot(g, wu[n])
        hid[:, pl.ds(pl.multiple_of(n * HALF, HALF), HALF)] = (jax.nn.gelu(gate, approximate=True) * up).astype(BF)
        return 0
    lax.fori_loop(0, 2, body, 0)


def down(hid, wd, n):
    return dot(hid[...], wd[n])


def layers_kernel(start, invf_in, norms_in, x_in, kl, vl, kg, vg, wq, wk, wv, wo, wg, wu, wd,
                  out_ref, k0_out, v0_out, k1_out, v1_out,
                  act, xres, kc, vc, qs, ks, vs, obuf, hid, pbuf, ds, dr, es, er, wgb, wub, wdb, wob, cosb, sinb, pa, pb, acc, tot, invf, norms,
                  ag_sem, d_sem, e_sem, g_sem, w_sem, o_sem, t_sem):
    p = Peers()
    copy_in = pltpu.make_async_copy
    qkv_loads = [[copy_in(w.at[l], buf.at[0, :, pl.ds(at, n)], w_sem.at[i]) for i, (w, at, n) in enumerate(((wq, 0, 512), (wk, 512, 256), (wv, 768, 256)))]
                 for l, buf in enumerate((wdb, wgb))]
    local_loads = [copy_in(kl, kc, w_sem.at[3]), copy_in(vl, vc, w_sem.at[4])]
    o_loads = [[copy_in(wo.at[l, :, pl.ds(n * HALF, HALF)], wob.at[n], w_sem.at[5 + n]) for n in PAIR] for l in PAIR]
    own = [copy_in(x_in.at[h], act.at[h, p.x, p.c], w_sem.at[7 + h]) for h in PAIR]
    mlp_loads = [[[copy_in(w.at[l, :, pl.ds(n * HALF, HALF)], buf.at[n], w_sem.at[9 + TWO * i + n]) for n in PAIR]
                  for i, (w, buf) in enumerate(((wg, wgb), (wu, wub), (wd, wdb)))] for l in PAIR]
    outs = [copy_in(src, dst, o_sem.at[i]) for i, (src, dst) in enumerate(((ks, k0_out), (vs, v0_out), (ks, k1_out), (vs, v1_out)))]

    def start_all(copies):
        for copy in copies:
            copy.start()

    def wait_all(copies):
        for copy in copies:
            copy.wait()

    params = [copy_in(invf_in, invf, o_sem.at[0]), copy_in(norms_in, norms, o_sem.at[1])]
    start_all(own + params)
    p.barrier()

    def ag_mate(h):
        view = act.at[h, p.x, p.c]
        return remote(view, view, ag_sem.at[0, 0, h], ag_sem.at[0, 1, h], p.mate)

    def ag_far(h):
        view = act.at[h, p.x, p.c]
        return remote(view, view, ag_sem.at[1, 0, h], ag_sem.at[1, 1, h], p.far)

    def ag_pass(h):
        view = act.at[h, 1 - p.x, p.c]
        return remote(view, view, ag_sem.at[2, 0, h], ag_sem.at[2, 1, h], p.mate)

    for h in PAIR:
        own[h].wait()
        ag_far(h).start()
        ag_mate(h).start()
    start_all(qkv_loads[0] + local_loads + o_loads[0])
    wait_all(params)

    for h in PAIR:
        pos = (lax.broadcasted_iota(jnp.int32, (TOK, 128), 0) + start[h]).astype(F32)
        angle = pos * invf[...]
        cosb[h] = jnp.cos(angle)
        sinb[h] = jnp.sin(angle)

    def scale(l, i):
        return 1.0 + norms[l, i:i + 1, :]

    def ag_arrive(h):
        ag_far(h).wait_recv()
        ag_pass(h).start()

    def ag_finish(h):
        ag_mate(h).wait_recv()
        ag_pass(h).wait()
        ag_mate(h).wait_send()
        ag_far(h).wait_send()
        xres[h] = act[h, :, p.c]
        norm_rows(act, h, scale(0, 0))

    def local_attention(h):
        q = qs[...]
        row = lax.broadcasted_iota(jnp.int32, (2 * TOK, 1), 0)
        i = jnp.where(row >= TOK, row - TOK, row)
        least = jnp.maximum(i + 1, WIN - start[h])
        acc = jnp.zeros((2 * TOK, HD), F32)
        total = jnp.zeros((2 * TOK, 1), F32)
        for b in PAIR:
            slot = lax.broadcasted_iota(jnp.int32, (1, 512), 1) + b * 512
            age = jnp.bitwise_and(slot - start[h], WIN - 1)
            wts = jnp.where(age >= least, soft_weights(dot_t(q, kc[h, b * 512:(b + 1) * 512, :])), 0.0)
            total += jnp.sum(wts, axis=-1, keepdims=True)
            acc += dot(wts.astype(BF), vc[h, b * 512:(b + 1) * 512, :])
        key = lax.broadcasted_iota(jnp.int32, (1, TOK), 1)
        wts = jnp.where(key <= i, soft_weights(dot_t(q, ks[h])), 0.0)
        total += jnp.sum(wts, axis=-1, keepdims=True)
        acc += dot(wts.astype(BF), vs[h])
        o = (acc / total).astype(BF)
        obuf[:, :HD] = o[:TOK]
        obuf[:, HD:] = o[TOK:]

    def exchange(s, er_slot, final=None):
        return Exchange(p, pbuf, ds, dr, es, er.at[er_slot], d_sem.at[s], e_sem.at[s], final)

    ex = [exchange(0, 0), exchange(1, 1), exchange(2, 0), exchange(3, 1)]
    sh = Shared(p, act, g_sem.at[1])

    def project(h, buf, q_dst):
        proj = dot(act[h].reshape(TOK, D), buf)
        rope_into(proj, cosb[h], sinb[h], q_dst, ks.at[h])
        vs[h] = proj[:, 768:].astype(BF)

    def first_attention():
        ag_arrive(0)
        for h in PAIR:
            ag_finish(h)
            if h == 0:
                wait_all(qkv_loads[0] + local_loads + o_loads[0])
                start_all(mlp_loads[0][0] + mlp_loads[0][1])
            project(h, wdb[0, :, :1024], qs)
            local_attention(h)
            for n in PAIR:
                ex[0].give(h, n, dot(obuf[...], wob[n]))
            if h == 0:
                ag_arrive(1)
            for n in PAIR:
                ex[0].send(h, n)
        start_all(mlp_loads[0][2] + outs[:2])

    def mlp(l):
        before, after = exchange(2 * l, 0), exchange(2 * l + 1, 1, l == 1)
        share = Shared(p, act, g_sem.at[2 * l])
        w_post, w_pre = scale(l, 1), scale(l, 2)
        before.take(0, xres, w_post, act, w_pre)
        share.copy(0).start()

        @pl.when(l == 1)
        def _():
            for n in PAIR:
                before.send(1, n)

        wait_all(mlp_loads[0][0] + mlp_loads[0][1])
        share.copy(0).wait()
        gate_up(act, 0, wgb, wub, hid)
        wait_all(mlp_loads[0][2])
        after.give(0, 0, down(hid, wdb, 0))
        before.take(1, xres, w_post, act, w_pre)
        share.copy(1).start()
        after.send(0, 0)
        after.give(0, 1, down(hid, wdb, 1))
        share.copy(1).wait()
        gate_up(act, 1, wgb, wub, hid, lambda: after.send(0, 1))
        for n in PAIR:
            after.give(1, n, down(hid, wdb, n))
        after.send(1, 0)

    def ring(a, g):
        s = lax.rem(g, 10)
        return wdb.at[s // 5, pl.ds(a * TILE, TILE), pl.ds(pl.multiple_of(lax.rem(s, 5) * HD, HD), HD)]

    def tile_in(a, g):
        src = (kg, vg)[a].at[g // NT, pl.ds(pl.multiple_of(lax.rem(g, NT) * TILE, TILE), TILE)]
        return pltpu.make_async_copy(src, ring(a, g), t_sem.at[a, g])

    def fetch(g):
        for a in PAIR:
            tile_in(a, g).wait()

        @pl.when(g + AHEAD < TWO * NT)
        def _():
            for a in PAIR:
                tile_in(a, g + AHEAD).start()

    row = lax.broadcasted_iota(jnp.int32, (2 * TOK, 1), 0)
    qi = jnp.where(row >= TOK, row - TOK, row)

    def global_attention(h):
        acc[...] = jnp.zeros_like(acc)
        tot[...] = jnp.zeros_like(tot)
        pb[...] = jnp.zeros_like(pb)
        base = h * NT

        def weigh(t, dst):
            keys = ring(0, base + t)
            for b in range(TILE // 256):
                scores = dot_t(qs[...], keys[b * 256:(b + 1) * 256, :])
                slot = lax.broadcasted_iota(jnp.int32, (1, 256), 1) + (t * TILE + b * 256)
                off = jnp.where(slot < start[h], S_OFF, HIDE)
                wts = jnp.exp2(jnp.tanh(scores * S_IN) * S_OUT - off)
                tot[...] += wts[:, :128] + wts[:, 128:]
                dst[:, b * 256:(b + 1) * 256] = wts.astype(BF)

        def four_tiles(i, _):
            t = 4 * i
            for j in range(4):
                fetch(base + t + j)
            part = dot(pb[...], ring(1, base + jnp.maximum(t - 1, 0))[...])
            for j, (dst, src) in enumerate(((pa, pa), (pb, pb), (pa, pa), (pb, None))):
                weigh(t + j, dst)
                if src is not None:
                    part += dot(src[...], ring(1, base + t + j)[...])
            acc[...] += part
            return 0

        lax.fori_loop(0, NT // 4, four_tiles, 0)
        before = dot(pb[...], ring(1, base + NT - 1)[...])
        wts = jnp.where(lax.broadcasted_iota(jnp.int32, (1, TOK), 1) <= qi, soft_weights(dot_t(qs[...], ks[h])), 0.0)
        total = jnp.sum(tot[...], axis=-1, keepdims=True) + jnp.sum(wts, axis=-1, keepdims=True)
        o = ((acc[...] + before + dot(wts.astype(BF), vs[h])) / total).astype(BF)
        obuf[:, :HD] = o[:TOK]
        obuf[:, HD:] = o[TOK:]

    def second_attention():
        start_all(qkv_loads[1])
        for g in range(AHEAD):
            for a in PAIR:
                tile_in(a, g).start()
        start_all(o_loads[1] + mlp_loads[1][1])
        ex[1].take(0, xres, scale(0, 3), act, scale(1, 0))
        sh.copy(0).start()
        ex[1].send(1, 1)
        wait_all(outs[:2] + qkv_loads[1])
        sh.copy(0).wait()
        project(0, wgb[0, :, :1024], qs)
        global_attention(0)
        ex[1].take(1, xres, scale(0, 3), act, scale(1, 0))
        sh.copy(1).start()
        wait_all(o_loads[1])
        for n in PAIR:
            ex[2].give(0, n, dot(obuf[...], wob[n]))
        ex[2].send(0, 0)
        sh.copy(1).wait()
        project(1, wgb[0, :, :1024], qs)
        ex[2].send(0, 1)
        start_all(mlp_loads[1][0])
        global_attention(1)
        for n in PAIR:
            ex[2].give(1, n, dot(obuf[...], wob[n]))
        start_all(outs[2:] + mlp_loads[1][2])

    def layer(l, _):
        pl.when(l == 0)(first_attention)
        pl.when(l == 1)(second_attention)
        mlp(l)
        return 0

    lax.fori_loop(0, 2, layer, 0)
    last = exchange(3, 1, True)
    last.take_final(0, xres, scale(1, 3), out_ref)
    last.send(1, 1)
    last.take_final(1, xres, scale(1, 3), out_ref)
    wait_all(outs[2:])


def shifted(ref, off, n):
    base = pl.multiple_of((off // 8) * 8, 8)
    rows = ref[pl.ds(base, n + 8), :]
    return pltpu.roll(rows, lax.rem(n + 8 - (off - base), n + 8), 0)[:n]


def cache_kernel(start, k_new, v_new, k0_new, v0_new, x_in, kl, vl, kg, vg,
                 x_out, kl_out, vl_out, kg_out, vg_out,
                 kb, vb, lbuf, ext, xbuf, fresh_rows, in_sem, out_sem, l_sem, f_sem):
    caches = ((kg, kb, kg_out, k_new), (vg, vb, vg_out, v_new))
    last = pl.ds(PAST, TOK)

    def tile(t):
        return pl.ds(pl.multiple_of(t * TILE, TILE), TILE)

    def rows_in(a, h, t, at):
        return pltpu.make_async_copy(caches[a][0].at[h, at], caches[a][1].at[h, at], in_sem.at[a, h, t])

    def rows_out(a, h, t, at):
        return pltpu.make_async_copy(caches[a][1].at[h, at], caches[a][2].at[h, at], out_sem.at[a, h, t])

    def each(h, body):
        lax.fori_loop(0, NT, lambda t, _: (body(h, t, tile(t)), 0)[1], 0)
        body(h, NT, last)

    def begin(h, t, at):
        for a in PAIR:
            rows_in(a, h, t, at).start()

    local = ((kl, k0_new, kl_out), (vl, v0_new, vl_out))
    for a in PAIR:
        pltpu.make_async_copy(local[a][0], lbuf.at[a], l_sem.at[a]).start()
    fresh_loads = [load(src, fresh_rows.at[i], f_sem.at[i]) for i, src in enumerate((k0_new, v0_new, k_new, v_new))]
    x_load = load(x_in, xbuf, l_sem.at[2])
    for h in PAIR:
        each(h, begin)

    def local_rows(a, h):
        fresh = fresh_rows[a, h].astype(F32)
        ext[0:TOK] = fresh
        ext[WIN:WIN + TOK] = fresh
        off = jnp.bitwise_and(-start[h], WIN - 1)

        def slots(b, _):
            lead = jnp.bitwise_and(b * 128 + off, WIN - 1)

            @pl.when((lead < TOK) | (lead > WIN - 128))
            def _():
                rows = shifted(ext, off + b * 128, 128)
                age = jnp.bitwise_and(lax.broadcasted_iota(jnp.int32, (128, 1), 0) + lead, WIN - 1)
                at = pl.ds(pl.multiple_of(b * 128, 128), 128)
                lbuf[a, h, at, :] = jnp.where(age < TOK, rows, lbuf[a, h, at, :].astype(F32)).astype(BF)

            return 0

        lax.fori_loop(0, WIN // 128, slots, 0)

    for copy in fresh_loads:
        copy.wait()
    for a in PAIR:
        pltpu.make_async_copy(local[a][0], lbuf.at[a], l_sem.at[a]).wait()
        for h in PAIR:
            local_rows(a, h)
        pltpu.make_async_copy(lbuf.at[a], local[a][2], l_sem.at[a]).start()
    x_load.wait()
    x_done = load(xbuf, x_out, l_sem.at[2])

    for h in PAIR:
        first = pl.multiple_of(jnp.minimum((start[h] // 16) * 16, CACHE - WROWS), 16)
        shift = first - start[h]

        def touched(t):
            return (t == first // TILE) | (t == (first + (WROWS - 1)) // TILE)

        def move(h, t, at):
            for a in PAIR:
                rows_in(a, h, t, at).wait()

            @pl.when(jnp.logical_not(touched(t)))
            def _():
                for a in PAIR:
                    rows_out(a, h, t, at).start()

        def move_touched(h, t, at):
            @pl.when(touched(t))
            def _():
                for a in PAIR:
                    rows_out(a, h, t, at).start()

        each(h, move)
        for a in PAIR:
            ext[16:16 + TOK] = fresh_rows[TWO + a, h].astype(F32)
            rows = shifted(ext, shift + 16, WROWS)
            idx = lax.broadcasted_iota(jnp.int32, (WROWS, 1), 0) + shift
            at = pl.ds(first, WROWS)
            buf = caches[a][1]
            buf[h, at, :] = jnp.where((idx >= 0) & (idx < TOK), rows, buf[h, at, :].astype(F32)).astype(BF)
        each(h, move_touched)

    def drain(h, t, at):
        for a in PAIR:
            rows_out(a, h, t, at).wait()

    for h in PAIR:
        each(h, drain)
    for a in PAIR:
        pltpu.make_async_copy(lbuf.at[a], local[a][2], l_sem.at[a]).wait()
    x_done.wait()


ANY = pl.BlockSpec(memory_space=pl.ANY)
VM = pl.BlockSpec(memory_space=pltpu.VMEM)
SM = pl.BlockSpec(memory_space=pltpu.SMEM)
DMA = pltpu.SemaphoreType.DMA


def vmem(*shape, dtype=BF):
    return pltpu.VMEM(shape, dtype)


def sds(*shape, dtype=BF):
    return jax.ShapeDtypeStruct(shape, dtype)


def run_layers(start, invf, norms, x, kl, vl, kg, vg, *weights):
    rows = sds(TWO, TOK, HD)
    pieces = vmem(TWO, TWO, TWO, BLK, HALF)
    return pl.pallas_call(
        layers_kernel,
        name="layers",
        out_shape=(sds(TWO, BLK, D), rows, rows, rows, rows),
        in_specs=[SM] + [ANY] * 14,
        out_specs=(VM, ANY, ANY, ANY, ANY),
        scratch_shapes=[
            vmem(TWO, TWO, TWO, BLK, D), vmem(TWO, TWO, BLK, D), vmem(TWO, WIN, HD), vmem(TWO, WIN, HD),
            vmem(TWO * TOK, HD), vmem(TWO, TOK, HD), vmem(TWO, TOK, HD),
            vmem(TOK, 512), vmem(TOK, D), vmem(TWO, TWO, TWO, BLK, HALF, dtype=F32),
            pieces, pieces, pieces, vmem(TWO, TWO, TWO, TWO, BLK, HALF),
            vmem(TWO, D, HALF), vmem(TWO, D, HALF), vmem(TWO, D, HALF), vmem(TWO, 512, HALF),
            vmem(TWO, TOK, 128, dtype=F32), vmem(TWO, TOK, 128, dtype=F32),
            vmem(TWO * TOK, TILE), vmem(TWO * TOK, TILE), vmem(TWO * TOK, HD, dtype=F32), vmem(TWO * TOK, 128, dtype=F32),
            vmem(1, 128, dtype=F32), vmem(TWO, 4, D, dtype=F32),
            DMA((3, TWO, TWO)), DMA((4, TWO, TWO, TWO)), DMA((4, TWO, TWO, TWO)), DMA((3, TWO, TWO)), DMA((15,)), DMA((4,)),
            DMA((TWO, TWO * NT)),
        ],
        compiler_params=pltpu.CompilerParams(collective_id=0, has_side_effects=True, vmem_limit_bytes=VMEM_LIMIT),
    )(start, invf, norms, x, kl, vl, kg, vg, *weights)


def run_caches(start, k_new, v_new, k0_new, v0_new, x, kl, vl, kg, vg):
    rows = vmem(TWO, CACHE, HD)
    return pl.pallas_call(
        cache_kernel,
        name="caches",
        out_shape=(sds(TWO, BLK, D), sds(TWO, WIN, HD), sds(TWO, WIN, HD), sds(TWO, CACHE, HD), sds(TWO, CACHE, HD)),
        in_specs=[SM] + [ANY] * 9,
        out_specs=(ANY,) * 5,
        scratch_shapes=[
            rows, rows, vmem(TWO, TWO, WIN, HD), vmem(TWO * WIN + 8, HD, dtype=F32), vmem(TWO, BLK, D), vmem(4, TWO, TOK, HD),
            DMA((TWO, TWO, NT + 1)), DMA((TWO, TWO, NT + 1)), DMA((3,)), DMA((4,)),
        ],
        compiler_params=pltpu.CompilerParams(has_side_effects=True, vmem_limit_bytes=VMEM_LIMIT),
    )(start, k_new, v_new, k0_new, v0_new, x, kl, vl, kg, vg)


def solution(mesh):
    act_spec = P('dp', 'tp', None)
    cache_spec = P('dp', None, 'tp', None)
    col_spec = P(None, None, 'tp')
    row_spec = P(None, 'tp', None)
    arg_specs = (act_spec, P('dp'), cache_spec, cache_spec, cache_spec, cache_spec, P(), col_spec, col_spec, col_spec, row_spec, col_spec, col_spec, row_spec)
    result_specs = (act_spec, cache_spec, cache_spec, cache_spec, cache_spec)
    inv_freq = np.power(np.float64(ROPE_BASE), np.arange(HD // 2) * (-2.0 / HD)).astype(np.float32)[None, :]

    def device_step(x, start, k_local, v_local, k_global, v_global, norms, w_q, w_k, w_v, w_o, w_gate, w_up, w_down):
        def flat(cache):
            return cache.reshape(cache.shape[0], cache.shape[1], cache.shape[3])

        kl, vl, kg, vg = flat(k_local), flat(v_local), flat(k_global), flat(v_global)
        invf = jnp.asarray(inv_freq)
        out, k0, v0, k1, v1 = run_layers(start, invf, norms, x, kl, vl, kg, vg, w_q, w_k, w_v, w_o, w_gate, w_up, w_down)
        out, kl_new, vl_new, kg_new, vg_new = run_caches(start, k1, v1, k0, v0, out, kl, vl, kg, vg)
        return (out, kl_new.reshape(k_local.shape), vl_new.reshape(v_local.shape), kg_new.reshape(k_global.shape), vg_new.reshape(v_global.shape))

    return jax.shard_map(device_step, mesh=mesh, in_specs=arg_specs, out_specs=result_specs, check_vma=False)
```

time: 144 us -> 140 us (0.972)
  Pallas kernels: 141 us -> 139 us
  local copies, waits for them, and re-layouts: 1.84 us -> 0 us
    pallas_call x1, Pallas kernels: 120 us -> 117 us  [run_layers(): pl.pallas_call(layers_kernel, name='layers', out_shape=(sds(TWO, BLK, D),...]
    unnamed x1 -> x0, local copies, waits for them, and re-layouts: 1.84 us -> none
where the time goes in v2:
time: 140 us
  Pallas kernels  139 us (99%)
    pallas_call x1, Pallas kernels, run_layers(): pl.pallas_call(layers_kernel, name='layers', out_shape=(sds(TWO, BLK, D),...  117 us
    pallas_call x1, Pallas kernels, run_caches(): pl.pallas_call(cache_kernel, name='caches', out_shape=(sds(TWO, BLK, D),...  21.7 us

profile of v2, /device:TPU:0, one launch (start us, length us, event | category | flops | bytes accessed | tf_op | source)
XLA Modules:
  0.0 139.6 jit_solution(14327646344126499679)
XLA Ops:
  0.6 117.3 %layers.1 = (bf16[2,48,2560]{2,1,0:T(8,128)(2,1)}, bf16[2,192,256]{2,1,0:T(8,128)(2,1)}, bf16[2,192,256]{2,1,0:T(8,128)(2,1)}, bf16[2,192,256]{2,1,0:T(8,128)(2,1)}, bf16[2,192,256]{2,1,0:T(8,128)(2,1)}) custom-call(s32[2]{0:T(128)} %start.3, f32[1,128]{1,0:T(1,128)} %constant.2.clone.invf_in, f32[2,4,2560]{2,1,0:T(4,128)} %norms_in.1, ...), custom_call_target="tpu_custom_call" | custom-call | tf_op jit(solution)/shard_map/layers/pallas_call | solution.py:556
  118.0 21.7 %caches.1 = (bf16[2,48,2560]{2,1,0:T(8,128)(2,1)}, bf16[2,1024,256]{2,1,0:T(8,128)(2,1)}, bf16[2,1024,256]{2,1,0:T(8,128)(2,1)}, bf16[2,12480,256]{2,1,0:T(8,128)(2,1)}, bf16[2,12480,256]{2,1,0:T(8,128)(2,1)}) custom-call(s32[2]{0:T(128)} %start.3, bf16[2,192,256]{2,1,0:T(8,128)(2,1)} %get-tuple-element.15.k_new, ...), custom_call_target="tpu_custom_call" | custom-call | tf_op jit(solution)/shard_map/caches/pallas_call | solution.py:580

commit v3 on v2

--- a/solution.py
+++ b/solution.py
@@ -324,6 +324,11 @@
         after.give(0, 1, down(hid, wdb, 1))
         share.copy(1).wait()
         gate_up(act, 1, wgb, wub, hid, lambda: after.send(0, 1))
+
+        @pl.when(l == 0)
+        def _():
+            start_all(qkv_loads[1] + mlp_loads[1][1])
+
         for n in PAIR:
             after.give(1, n, down(hid, wdb, n))
         after.send(1, 0)
@@ -385,11 +390,10 @@
         obuf[:, HD:] = o[TOK:]
 
     def second_attention():
-        start_all(qkv_loads[1])
         for g in range(AHEAD):
             for a in PAIR:
                 tile_in(a, g).start()
-        start_all(o_loads[1] + mlp_loads[1][1])
+        start_all(o_loads[1])
         ex[1].take(0, xres, scale(0, 3), act, scale(1, 0))
         sh.copy(0).start()
         ex[1].send(1, 1)

time: 140 us -> 137 us (0.979)
  Pallas kernels: 139 us -> 137 us
    pallas_call x1, Pallas kernels: 117 us -> 115 us  [run_layers(): pl.pallas_call(layers_kernel, name='layers', out_shape=(sds(TWO, BLK, D),...]
where the time goes in v3:
time: 137 us
  Pallas kernels  137 us (100%)
    pallas_call x1, Pallas kernels, run_layers(): pl.pallas_call(layers_kernel, name='layers', out_shape=(sds(TWO, BLK, D),...  115 us
    pallas_call x1, Pallas kernels, run_caches(): pl.pallas_call(cache_kernel, name='caches', out_shape=(sds(TWO, BLK, D),...  21.3 us

profile of v3, /device:TPU:0, one launch (start us, length us, event | category | flops | bytes accessed | tf_op | source)
XLA Modules:
  0.0 137.2 jit_solution(17709260848932618836)
XLA Ops:
  0.6 115.3 %layers.1 = (bf16[2,48,2560]{2,1,0:T(8,128)(2,1)}, bf16[2,192,256]{2,1,0:T(8,128)(2,1)}, bf16[2,192,256]{2,1,0:T(8,128)(2,1)}, bf16[2,192,256]{2,1,0:T(8,128)(2,1)}, bf16[2,192,256]{2,1,0:T(8,128)(2,1)}) custom-call(s32[2]{0:T(128)} %start.3, f32[1,128]{1,0:T(1,128)} %constant.2.clone.invf_in, f32[2,4,2560]{2,1,0:T(4,128)} %norms_in.1, ...), custom_call_target="tpu_custom_call" | custom-call | tf_op jit(solution)/shard_map/layers/pallas_call | solution.py:560
  116.0 21.3 %caches.1 = (bf16[2,48,2560]{2,1,0:T(8,128)(2,1)}, bf16[2,1024,256]{2,1,0:T(8,128)(2,1)}, bf16[2,1024,256]{2,1,0:T(8,128)(2,1)}, bf16[2,12480,256]{2,1,0:T(8,128)(2,1)}, bf16[2,12480,256]{2,1,0:T(8,128)(2,1)}) custom-call(s32[2]{0:T(128)} %start.3, bf16[2,192,256]{2,1,0:T(8,128)(2,1)} %get-tuple-element.15.k_new, ...), custom_call_target="tpu_custom_call" | custom-call | tf_op jit(solution)/shard_map/caches/pallas_call | solution.py:584
